TPU v7x, 32 devices: a whole 2x2x4 slice. The times are simulated.
32 devices in a mesh: fsdp: 2 (over x), context: 4 (over z), tensor: 4 (over y, core).
Axes of the slice: x: 2, y: 2, z: 4, core: 2. Of those that a mesh axis runs over, the one named last changes fastest.
Arguments:
- activations: bfloat16 [2, 2048, 1152], P('fsdp', 'context'), may hold values from -6 to 6
- positions: int32 [2, 2048], P('fsdp', 'context'), may hold values from 0 to 2047, as said below
- seg_ids: int32 [2, 2048], P('fsdp', 'context'), may hold values from 0 to 3, as said below
- norm_gains: bfloat16 [4, 1152], P(None, ('fsdp', 'context')), may hold values from 0.5 to 1.5
- head_gains: bfloat16 [2, 256], P(None, ('fsdp', 'context')), may hold values from 0.25 to 1.75
- w_query: bfloat16 [1152, 1024], P(('fsdp', 'context'), 'tensor'), may hold values from -0.1875 to 0.1875
- w_keyval: bfloat16 [1152, 512], P(('fsdp', 'context')), may hold values from -0.1875 to 0.1875
- w_out: bfloat16 [1152, 1024], P(('fsdp', 'context'), 'tensor'), may hold values from -0.1875 to 0.1875
- w_gateup: bfloat16 [1152, 2, 6912], P(('fsdp', 'context'), None, 'tensor'), may hold values from -0.1875 to 0.1875
- w_down: bfloat16 [1152, 6912], P(('fsdp', 'context'), 'tensor'), may hold values from -0.078125 to 0.078125
- cotangent: bfloat16 [2, 2048, 1152], P('fsdp', 'context'), may hold values from -6 to 6
Outputs:
- block_output: bfloat16 [2, 2048, 1152], P('fsdp', 'context')
- input_grad: bfloat16 [2, 2048, 1152], P('fsdp', 'context')
- norm_gains_grad: float32 [4, 1152], P(None, ('fsdp', 'context'))
- head_gains_grad: float32 [2, 256], P(None, ('fsdp', 'context'))
- w_query_grad: float32 [1152, 1024], P(('fsdp', 'context'), 'tensor')
- w_keyval_grad: float32 [1152, 512], P(('fsdp', 'context'))
- w_out_grad: float32 [1152, 1024], P(('fsdp', 'context'), 'tensor')
- w_gateup_grad: float32 [1152, 2, 6912], P(('fsdp', 'context'), None, 'tensor')
- w_down_grad: float32 [1152, 6912], P(('fsdp', 'context'), 'tensor')
Inputs may be any that keep to these rules, and one draw needn't show every extreme that they name: `positions`: within a sequence, a document is a run of consecutive tokens with one document number; numbers never fall along a sequence. Positions are 0 at a document's first token and rise by one from token to token inside it. The first sequence is one document. `seg_ids`: document numbers of a sequence start at 0 and never fall along it.
All inputs are finite; a program needn't handle non-finite values.
Results may differ from a plain program's by a relative error of at most 0.024.
Values may be sent and summed in bfloat16 or wider, within the bound.
A program may use at most 192 MiB of HBM per device.

v0:
```python
import jax
import jax.numpy as jnp
from jax import lax
from jax.sharding import PartitionSpec as P

HD = 256
WINDOW = 512


EPSILON = 1e-06


def from_behind(block, axis, distance):
    devices = range(lax.axis_size(axis))
    route = [(i - distance, i) for i in devices if i - distance in devices]
    return lax.ppermute(block, axis, route)


def rms_norm(values, gain):
    factor = lax.rsqrt(jnp.mean(values * values, axis=-1, keepdims=True) + EPSILON)
    return values * factor * gain


def rotate(tensor, places):
    width_all = tensor.shape[-1]
    half_width = width_all // 2
    freqs = jnp.power(10000.0, -jnp.arange(half_width, dtype=jnp.float32) * 2.0 / width_all)
    angles = places.astype(jnp.float32)[:, None] * freqs[None, :]
    cosine = jnp.cos(angles)[:, None, :]
    sine = jnp.sin(angles)[:, None, :]
    first_half = tensor[..., :half_width]
    second_half = tensor[..., half_width:]
    return jnp.concatenate(
        [first_half * cosine - second_half * sine, second_half * cosine + first_half * sine],
        axis=-1,
    )


def glu(gate_up):
    return jax.nn.gelu(gate_up[:, 0], approximate=True) * gate_up[:, 1]


def contract_last(left_side, right_side):
    return lax.dot_general(
        left_side, right_side, (((1,), (1,)), ((), ())), preferred_element_type=jnp.float32
    )


def contract_first(left_side, right_side):
    return lax.dot_general(
        left_side, right_side, (((0,), (0,)), ((), ())), preferred_element_type=jnp.float32
    )


def shards(
    activations,
    positions,
    seg_ids,
    norm_gains,
    head_gains,
    w_query,
    w_keyval,
    w_out,
    w_gateup,
    w_down,
    cotangent,
):
    tokens = activations.shape[1]
    local_heads = w_query.shape[1] // HD
    inputs = activations[0].astype(jnp.float32)
    places = positions[0]
    documents = seg_ids[0]
    gains_all, heads_all, query_all, keyval_all, out_all = (
        lax.all_gather(norm_gains, ("fsdp", "context"), axis=1, tiled=True),
        lax.all_gather(head_gains, ("fsdp", "context"), axis=1, tiled=True),
        lax.all_gather(w_query, ("fsdp", "context"), axis=0, tiled=True),
        lax.all_gather(w_keyval, ("fsdp", "context"), axis=0, tiled=True),
        lax.all_gather(w_out, ("fsdp", "context"), axis=0, tiled=True),
    )
    gains_f = gains_all.astype(jnp.float32)
    heads_f = heads_all.astype(jnp.float32)
    normed_f, input_back = jax.vjp(rms_norm, inputs, gains_f[0])
    normed = normed_f.astype(jnp.bfloat16)
    query_raw = jnp.dot(normed, query_all, preferred_element_type=jnp.float32).reshape(
        tokens, local_heads, HD
    )
    keyval_raw = jnp.dot(normed, keyval_all, preferred_element_type=jnp.float32)

    def prepare(raw_heads, head_gain):
        return rotate(rms_norm(raw_heads, head_gain), places)

    query_rot, query_back = jax.vjp(prepare, query_raw, heads_f[0])
    key_rot, key_back = jax.vjp(prepare, keyval_raw[:, None, :HD], heads_f[1])
    queries = query_rot.astype(jnp.bfloat16)
    own_keyval = jnp.concatenate([key_rot[:, 0], keyval_raw[:, HD:]], axis=1).astype(jnp.bfloat16)
    labels = jnp.stack([places, documents])
    keep_from = tokens - tokens
    left_keyval, left_labels = from_behind((own_keyval, labels), "context", 1)
    keys_all = jnp.concatenate([left_keyval, own_keyval], axis=0)
    key_places = jnp.concatenate([left_labels[0], places])
    key_documents = jnp.concatenate([left_labels[1], documents])
    has_left = lax.axis_index("context") > 0
    key_live = jnp.concatenate([jnp.full((tokens,), has_left), jnp.ones((tokens,), dtype=bool)])
    scale_factor = HD ** (-0.5)
    block_rows = 512
    block_starts = jnp.arange(tokens // block_rows) * block_rows

    def block_scores():
        spacing = places[:, None] - key_places[None, :]
        visible = (
            key_live[None, :]
            & (documents[:, None] == key_documents[None, :])
            & (spacing >= 0)
            & (spacing < WINDOW)
        )
        raw_scores = (
            jnp.einsum("qhd,kd->hqk", queries, keys_all[:, :HD], preferred_element_type=jnp.float32)
            * scale_factor
        )
        return (jnp.where(visible[None], raw_scores, -1e30), keys_all, queries)

    def forward_block(start):
        scores, near_keyval, query_block = block_scores()
        row_top = jnp.max(scores, axis=-1, keepdims=True)
        raised = jnp.exp(scores - row_top)
        row_total = jnp.sum(raised, axis=-1, keepdims=True)
        probs = raised / row_total
        mixed_block = jnp.einsum(
            "hqk,kd->qhd",
            probs.astype(jnp.bfloat16),
            near_keyval[:, HD:],
            preferred_element_type=jnp.float32,
        )
        return (mixed_block.astype(jnp.bfloat16), row_top + jnp.log(row_total))

    mixed_blocks, log_blocks = lax.map(forward_block, block_starts)
    mixed_low = mixed_blocks.reshape(tokens, local_heads * HD)
    branch = lax.psum(contract_last(mixed_low, out_all), "tensor")
    post_attn, post_attn_back = jax.vjp(rms_norm, branch, gains_f[1])
    hidden = inputs + post_attn
    normed_mlp_f, pre_mlp_back = jax.vjp(rms_norm, hidden, gains_f[2])
    normed_mlp = normed_mlp_f.astype(jnp.bfloat16)
    columns = normed_mlp
    gate_up = jnp.einsum(
        "bn,nkf->bkf",
        columns,
        lax.all_gather(w_gateup, ("fsdp", "context"), axis=0, tiled=True),
        preferred_element_type=jnp.float32,
    )
    active_f, glu_back = jax.vjp(glu, gate_up)
    active = active_f.astype(jnp.bfloat16)
    down = lax.psum(
        contract_last(
            active, lax.all_gather(w_down, ("fsdp", "context"), axis=0, tiled=True)
        ).astype(jnp.bfloat16),
        "tensor",
    ).astype(jnp.float32)
    post_mlp, post_mlp_back = jax.vjp(rms_norm, down, gains_f[3])
    result = hidden + post_mlp
    grad_out = cotangent[0].astype(jnp.float32)
    d_down, gain_post_mlp = post_mlp_back(grad_out)
    down_low = d_down.astype(jnp.bfloat16)
    columns = down_low
    d_active = jnp.dot(
        columns,
        lax.all_gather(w_down, ("fsdp", "context"), axis=0, tiled=True),
        preferred_element_type=jnp.float32,
    )
    d_gate_up = glu_back(d_active)[0].astype(jnp.bfloat16)
    d_normed_part = jnp.einsum(
        "bkf,nkf->bn",
        d_gate_up,
        lax.all_gather(w_gateup, ("fsdp", "context"), axis=0, tiled=True),
        preferred_element_type=jnp.float32,
    )
    d_normed_mlp = lax.psum(d_normed_part.astype(jnp.bfloat16), "tensor").astype(jnp.float32)
    d_hidden_norm, gain_pre_mlp = pre_mlp_back(d_normed_mlp)
    d_hidden = grad_out + d_hidden_norm
    features = normed_mlp
    grad_cols = down_low
    gate_up_term = jnp.einsum(
        "bn,bkf->nkf", features, d_gate_up, preferred_element_type=jnp.float32
    )
    down_term = contract_first(grad_cols, active)
    mlp_grads = lax.psum_scatter(
        jnp.concatenate([gate_up_term, down_term[:, None, :]], axis=1).astype(jnp.bfloat16),
        ("fsdp", "context"),
        scatter_dimension=0,
        tiled=True,
    ).astype(jnp.float32)
    d_branch, gain_post_attn = post_attn_back(d_hidden)
    branch_low = d_branch.astype(jnp.bfloat16)
    d_mixed = jnp.dot(branch_low, out_all, preferred_element_type=jnp.float32)
    d_mixed_low = d_mixed.astype(jnp.bfloat16).reshape(tokens, local_heads, HD)

    def backward_block(carry, item):
        start, log_block = item
        scores, near_keyval, query_block = block_scores()
        probs_again = jnp.exp(scores - log_block)
        d_probs = jnp.einsum(
            "qhd,kd->hqk", d_mixed_low, near_keyval[:, HD:], preferred_element_type=jnp.float32
        )
        row_inner = jnp.sum(probs_again * d_probs, axis=-1, keepdims=True)
        d_scores = (probs_again * (d_probs - row_inner)).astype(jnp.bfloat16)
        d_query_block = (
            jnp.einsum(
                "hqk,kd->qhd", d_scores, near_keyval[:, :HD], preferred_element_type=jnp.float32
            )
            * scale_factor
        )
        d_keys = (
            jnp.einsum("hqk,qhd->kd", d_scores, query_block, preferred_element_type=jnp.float32)
            * scale_factor
        )
        d_values = jnp.einsum(
            "hqk,qhd->kd",
            probs_again.astype(jnp.bfloat16),
            d_mixed_low,
            preferred_element_type=jnp.float32,
        )
        updated = carry + jnp.concatenate([d_keys, d_values], axis=1)
        return (updated, d_query_block)

    d_keyval, d_query_blocks = lax.scan(
        backward_block,
        jnp.zeros((tokens + tokens, 2 * HD), jnp.float32),
        (block_starts, log_blocks),
    )
    d_queries = d_query_blocks.reshape(tokens, local_heads, HD)
    returned = from_behind(d_keyval[:tokens].astype(jnp.bfloat16), "context", -1).astype(
        jnp.float32
    )
    own_grad = d_keyval[tokens:].at[keep_from:].add(returned)
    d_query_raw, gain_query = query_back(d_queries)
    d_query_low = d_query_raw.reshape(tokens, local_heads * HD).astype(jnp.bfloat16)
    d_normed_query, keyval_grad, gain_query_all = (
        lax.psum(contract_last(d_query_low, query_all).astype(jnp.bfloat16), "tensor").astype(
            jnp.float32
        ),
        lax.psum(own_grad.astype(jnp.bfloat16), "tensor").astype(jnp.float32),
        lax.psum(gain_query.astype(jnp.bfloat16), "tensor").astype(jnp.float32),
    )
    d_key_raw, gain_key = key_back(keyval_grad[:, None, :HD])
    d_keyval_low = jnp.concatenate([d_key_raw[:, 0], keyval_grad[:, HD:]], axis=1).astype(
        jnp.bfloat16
    )
    d_normed = d_normed_query + contract_last(d_keyval_low, keyval_all)
    d_input_norm, gain_input = input_back(d_normed)
    input_total = d_hidden + d_input_norm
    features = normed
    grad_cols = branch_low
    attn_grads = lax.psum_scatter(
        jnp.stack(
            [contract_first(features, d_query_low), contract_first(grad_cols, mixed_low)], axis=1
        ).astype(jnp.bfloat16),
        ("fsdp", "context"),
        scatter_dimension=0,
        tiled=True,
    ).astype(jnp.float32)
    keyval_term = contract_first(normed, d_keyval_low)
    gain_terms = jnp.stack([gain_input, gain_post_attn, gain_pre_mlp, gain_post_mlp])
    head_terms = jnp.stack([gain_query_all, gain_key])
    gain_grad, head_grad, keyval_weight_grad = (
        lax.psum_scatter(
            gain_terms.astype(jnp.bfloat16), ("fsdp", "context"), scatter_dimension=1, tiled=True
        ).astype(jnp.float32),
        lax.psum_scatter(
            head_terms.astype(jnp.bfloat16), ("fsdp", "context"), scatter_dimension=1, tiled=True
        ).astype(jnp.float32),
        lax.psum_scatter(
            keyval_term.astype(jnp.bfloat16), ("fsdp", "context"), scatter_dimension=0, tiled=True
        ).astype(jnp.float32),
    )
    return (
        result[None].astype(jnp.bfloat16),
        input_total[None].astype(jnp.bfloat16),
        gain_grad,
        head_grad,
        attn_grads[:, 0],
        keyval_weight_grad,
        attn_grads[:, 1],
        mlp_grads[:, :2],
        mlp_grads[:, 2],
    )


def solution(mesh):
    return jax.shard_map(
        shards,
        mesh=mesh,
        in_specs=(
            P("fsdp", "context", None),
            P("fsdp", "context"),
            P("fsdp", "context"),
            P(None, ("fsdp", "context")),
            P(None, ("fsdp", "context")),
            P(("fsdp", "context"), "tensor"),
            P(("fsdp", "context"), None),
            P(("fsdp", "context"), "tensor"),
            P(("fsdp", "context"), None, "tensor"),
            P(("fsdp", "context"), "tensor"),
            P("fsdp", "context", None),
        ),
        out_specs=(
            P("fsdp", "context", None),
            P("fsdp", "context", None),
            P(None, ("fsdp", "context")),
            P(None, ("fsdp", "context")),
            P(("fsdp", "context"), "tensor"),
            P(("fsdp", "context"), None),
            P(("fsdp", "context"), "tensor"),
            P(("fsdp", "context"), None, "tensor"),
            P(("fsdp", "context"), "tensor"),
        ),
        check_vma=False,
    )
```

profile of v0, /device:TPU:0, one launch (start us, length us, event | category | flops | bytes accessed | tf_op | source)
XLA Modules:
  0.0 1370.5 jit_solution(6977014308560481948)
XLA Ops:
  8.7 4.9 collective-permute-start.1
  14.3 18.8 %all-gather.1 = bf16[8,32,2]{1,2,0:T(2,128)(2,1)S(1)} all-gather(bf16[1,32,2]{1,2,0:T(2,128)(2,1)} %bitcast.247), channel_id=1, replica_groups=mesh['fsdp'=2,'context'=4,'tensor'=4] {'fsdp','context'}, dimensions={0}, use_global_device_ids=true | all-gather | bytes 1152 | tf_op jit(solution)/shard_map/all_gather | solution.py:75
  33.2 27.2 %all-gather = bf16[8,144,4]{1,2,0:T(4,128)(2,1)S(1)} all-gather(bf16[1,144,4]{1,2,0:T(4,128)(2,1)} %bitcast.246), channel_id=1, replica_groups=mesh['fsdp'=2,'context'=4,'tensor'=4] {'fsdp','context'}, dimensions={0}, use_global_device_ids=true | all-gather | bytes 10368 | tf_op jit(solution)/shard_map/all_gather | solution.py:74
  62.8 32.6 %all_gather.26 = bf16[1152,256]{1,0:T(8,128)(2,1)S(1)} all-gather(bf16[144,256]{1,0:T(8,128)(2,1)} %param.20), channel_id=1, replica_groups=mesh['fsdp'=2,'context'=4,'tensor'=4] {'fsdp','context'}, dimensions={0}, use_global_device_ids=true | all-gather | bytes 663552 | tf_op jit(solution)/shard_map/all_gather | solution.py:76
  96.3 2.0 multiply_reduce_fusion.4
  99.2 2.2 fusion.127
  101.8 1.9 fusion.108
  103.8 2.1 collective-permute-start
  105.9 32.7 %all_gather.27 = bf16[1152,256]{1,0:T(8,128)(2,1)S(1)} all-gather(bf16[144,256]{1,0:T(8,128)(2,1)S(1)} %copy-done.37), channel_id=1, replica_groups=mesh['fsdp'=2,'context'=4,'tensor'=4] {'fsdp','context'}, dimensions={0}, use_global_device_ids=true | all-gather | bytes 663552 | tf_op jit(solution)/shard_map/all_gather | solution.py:78
  140.0 2.2 fusion.135
  143.6 2.1 fusion.138
  148.0 55.3 %all-reduce.15.cloned.1.call-done = f32[512,1152]{1,0:T(8,128)} async-done(((f32[512,1152]{1,0:T(8,128)}), f32[512,1152]{1,0:T(8,128)}) %all-reduce.15.cloned.1.call-update) | async-done | bytes 2359312 | tf_op jit(solution)/shard_map/psum | solution.py:138
  203.4 2.0 multiply_reduce_fusion.3
  206.0 2.0 multiply_reduce_fusion.2
  208.5 120.5 %all-gather.8.cloned.1.call-done = bf16[1152,2,1728]{2,0,1:T(8,128)(2,1)} async-done(((bf16[144,2,1728]{2,0,1:T(8,128)(2,1)}), bf16[1152,2,1728]{2,0,1:T(8,128)(2,1)}) %all-gather.8.cloned.1.call-update) | async-done | bytes 7962640 | tf_op jit(solution)/shard_map/all_gather | solution.py:147
  329.0 8.3 fusion.110
  337.3 2.9 copy-done.11
  340.2 2.4 multiply_convert_fusion
  342.7 58.4 %all-gather.10.cloned.1.call-done = bf16[1152,1728]{1,0:T(8,128)(2,1)} async-done(((bf16[144,1728]{1,0:T(8,128)(2,1)}), bf16[1152,1728]{1,0:T(8,128)(2,1)}) %all-gather.10.cloned.1.call-update) | async-done | bytes 3981328 | tf_op jit(solution)/shard_map/all_gather | solution.py:154
  401.1 6.3 convolution_convert_fusion.4
  407.6 36.1 %all-reduce.17.cloned.1.call-done = bf16[512,1152]{1,0:T(8,128)(2,1)} async-done(((bf16[512,1152]{1,0:T(8,128)(2,1)}), bf16[512,1152]{1,0:T(8,128)(2,1)}) %all-reduce.17.cloned.1.call-update) | async-done | bytes 1179664 | tf_op jit(solution)/shard_map/psum | solution.py:152
  443.7 1.7 fusion.37
  445.4 3.4 fusion.36
  448.8 11.4 multiply_bitcast_fusion
  460.2 1.7 copy-done.85
  462.0 8.1 fusion.8
  471.6 36.3 %all-reduce.19.cloned.1.call-done = bf16[512,1152]{1,0:T(8,128)(2,1)} async-done(((bf16[512,1152]{1,0:T(8,128)(2,1)}), bf16[512,1152]{1,0:T(8,128)(2,1)}) %all-reduce.19.cloned.1.call-update) | async-done | bytes 1179664 | tf_op jit(solution)/shard_map/psum | solution.py:176
  508.0 3.5 fusion.27
  511.6 4.5 multiply_reduce_fusion
  527.6 11.6 collective-permute-done.2
  544.0 7.0 psum.47
  551.1 2.3 fusion.21
  553.4 2.6 fusion.20
  555.9 28.6 %all-reduce.23.cloned.1.call-done = (bf16[512,1152]{1,0:T(8,128)(2,1)}, bf16[512,512]{0,1:T(8,128)(2,1)}) async-done(((bf16[512,1152]{1,0:T(8,128)(2,1)}, bf16[512,512]{0,1:T(8,128)(2,1)}), (bf16[512,1152]{1,0:T(8,128)(2,1)}, bf16[512,512]{0,1:T(8,128)(2,1)})) %all-reduce.23.cloned.1.call-update) | async-done | bytes 1703952 | tf_op jit(solution)/shard_map/psum | solution.py:237
  587.5 3.3 fusion.25
  598.0 3.1 convolution_convert_fusion.2
  601.2 6.6 fusion
  607.7 9.4 convolution_convert_fusion
  617.1 7.5 pad_maximum_fusion
  624.6 27.1 %copy.35 = bf16[1152,3,1728]{2,1,0:T(4,128)(2,1)} copy(bf16[1152,3,1728]{0,2,1:T(8,128)(2,1)} %pad_maximum_fusion) | data formatting | bytes 23887872 | tf_op jit(solution)/shard_map/concatenate | solution.py:186
  654.5 3.3 fusion.48
  659.2 58.9 %reduce-scatter.13.cloned.1.call-done = bf16[144,4]{1,0:T(8,128)(2,1)} async-done(((bf16[1152,4]{1,0:T(8,128)(2,1)}), bf16[144,4]{1,0:T(8,128)(2,1)}) %reduce-scatter.13.cloned.1.call-update) | async-done | bytes 1168
  719.5 65.4 %reduce-scatter.9.cloned.1.call-done = bf16[144,2,256]{2,0,1:T(8,128)(2,1)} async-done(((bf16[1152,2,256]{2,0,1:T(8,128)(2,1)}), bf16[144,2,256]{2,0,1:T(8,128)(2,1)}) %reduce-scatter.9.cloned.1.call-update) | async-done | bytes 147472 | tf_op jit(solution)/shard_map/reduce_scatter | solution.py:252
  786.6 65.4 %reduce-scatter.11.cloned.1.call-done = bf16[144,512]{1,0:T(8,128)(2,1)} async-done(((bf16[1152,512]{1,0:T(8,128)(2,1)}), bf16[144,512]{1,0:T(8,128)(2,1)}) %reduce-scatter.11.cloned.1.call-update) | async-done | bytes 147472 | tf_op jit(solution)/shard_map/reduce_scatter | solution.py:270
  852.0 1.7 convert_element_type.197
  853.6 503.4 %all-reduce.21.cloned.1.call-done = bf16[1152,3,1728]{2,1,0:T(4,128)(2,1)} async-done(((bf16[1152,3,1728]{2,1,0:T(4,128)(2,1)}), bf16[1152,3,1728]{2,1,0:T(4,128)(2,1)}) %all-reduce.21.cloned.1.call-update) | async-done | bytes 11943952
  1357.0 2.1 dynamic-slice_convert_fusion
  1360.2 2.0 slice.153
  (278 shorter events, 49.3 us)
Async XLA Ops:
  7.2 92.0 %all-gather.6.cloned.1.call-start = ((), (), s32[]{:S(2)}) async-start(), calls=%async_computation.4 | async-start | bytes 1327104 | tf_op jit(solution)/shard_map/all_gather | solution.py:77
  7.9 195.5 %all-reduce.15.cloned.1.call-start = ((), (), s32[]{:S(2)}) async-start(), calls=%async_computation.5 | async-start | bytes 4718592 | tf_op jit(solution)/shard_map/psum | solution.py:138
  8.7 130.0 %collective-permute-start.1 = (s32[2,512]{1,0:T(2,128)S(1)}, s32[2,512]{1,0:T(2,128)S(1)}, u32[]{:S(2)}, u32[]{:S(2)}) collective-permute-start(s32[2,512]{1,0:T(2,128)S(1)} %pad_add_fusion.2), channel_id=1, source_target_pairs={{0,4},{4,8},{8,12},{1,5},{5,9},{9,13},{2,6},{6,10},{10,14},{3,7},{... | collective-permute-start | bytes 12296 | tf_op jit(solution)/shard_map/ppermute | solution.py:16
  14.3 87.5 %copy-start.41 = (f32[512]{0:T(512)}, f32[512]{0:T(512)S(1)}, u32[]{:S(2)}) copy-start(f32[512]{0:T(512)S(1)} %convert_element_type.160) | copy-start | bytes 6148
  60.5 41.3 %copy-start.78 = (f32[128]{0:T(128)}, f32[128]{0:T(128)S(1)}, u32[]{:S(2)}) copy-start(f32[128]{0:T(128)S(1)} %multiply_power_fusion) | copy-start | bytes 1540
  61.1 38.1 %copy-start.47 = (f32[1152]{0:T(1024)}, f32[1152]{0:T(1024)S(1)}, u32[]{:S(2)}) copy-start(f32[1152]{0:T(1024)S(1)} %get-tuple-element.128) | copy-start | bytes 13828
  62.7 35.5 %copy-start.57 = (f32[512]{0:T(512)}, f32[512]{0:T(512)S(1)}, u32[]{:S(2)}) copy-start(f32[512]{0:T(512)S(1)} %fusion.28) | copy-start | bytes 6148
  62.7 36.5 %copy-start.75 = (f32[512]{0:T(512)}, f32[512]{0:T(512)S(1)}, u32[]{:S(2)}) copy-start(f32[512]{0:T(512)S(1)} %fusion.112) | copy-start | bytes 6148
  62.7 36.4 %copy-start.68 = (f32[1,256]{1,0:T(1,128)}, f32[1,256]{1,0:T(1,128)S(1)}, u32[]{:S(2)}) copy-start(f32[1,256]{1,0:T(1,128)S(1)} %get-tuple-element.153) | copy-start | bytes 3076
  62.7 38.9 %copy-start.66 = (f32[1,256]{1,0:T(1,128)}, f32[1,256]{1,0:T(1,128)S(1)}, u32[]{:S(2)}) copy-start(f32[1,256]{1,0:T(1,128)S(1)} %get-tuple-element.154) | copy-start | bytes 3076
  62.8 36.5 %copy-start.8 = (bf16[1,512,1152]{2,1,0:T(8,128)(2,1)S(1)}, bf16[1,512,1152]{2,1,0:T(8,128)(2,1)}, u32[]{:S(2)}) copy-start(bf16[1,512,1152]{2,1,0:T(8,128)(2,1)} %param.15) | copy-start | bytes 3538948
  101.7 37.0 %copy-start.43 = (f32[512]{0:T(512)}, f32[512]{0:T(512)S(1)}, u32[]{:S(2)}) copy-start(f32[512]{0:T(512)S(1)} %fusion.113) | copy-start | bytes 6148
  101.7 37.0 %copy-start.62 = (s32[1,512]{1,0:T(1,128)S(1)}, s32[1,512]{1,0:T(1,128)}, u32[]{:S(2)}) copy-start(s32[1,512]{1,0:T(1,128)} %param.16) | copy-start | bytes 6148
  101.7 37.0 %copy-start.72 = (s32[1,512]{1,0:T(1,128)S(1)}, s32[1,512]{1,0:T(1,128)}, u32[]{:S(2)}) copy-start(s32[1,512]{1,0:T(1,128)} %param.17) | copy-start | bytes 6148
  103.7 38.6 %copy-start.30 = (bf16[512,128]{0,1:T(8,128)(2,1)}, bf16[512,128]{0,1:T(8,128)(2,1)S(1)}, u32[]{:S(2)}) copy-start(bf16[512,128]{0,1:T(8,128)(2,1)S(1)} %get-tuple-element.141) | copy-start | bytes 393220
  103.8 34.9 %collective-permute-start = (bf16[512,512]{0,1:T(8,128)(2,1)S(1)}, bf16[512,512]{0,1:T(8,128)(2,1)}, u32[]{:S(2)}, u32[]{:S(2)}) collective-permute-start(bf16[512,512]{0,1:T(8,128)(2,1)S(1)} %pad_maximum_fusion.3), channel_id=1, source_target_pairs={{0,4},{4,8},{8,12},{1,5},{5,9},{9,13},{2,6},{6,10},{10,14},{3,7},{... | collective-permute-start | bytes 1572872 | tf_op jit(solution)/shard_map/ppermute | solution.py:16
  145.7 183.3 %all-gather.8.cloned.1.call-start = ((), (), s32[]{:S(2)}) async-start(), calls=%async_computation.6 | async-start | bytes 9289728 | tf_op jit(solution)/shard_map/all_gather | solution.py:147
  146.9 254.2 %all-gather.10.cloned.1.call-start = ((), (), s32[]{:S(2)}) async-start(), calls=%async_computation.7 | async-start | bytes 4644864 | tf_op jit(solution)/shard_map/all_gather | solution.py:154
  147.4 296.3 %all-reduce.17.cloned.1.call-start = ((), (), s32[]{:S(2)}) async-start(), calls=%async_computation.8 | async-start | bytes 2359296 | tf_op jit(solution)/shard_map/psum | solution.py:152
  208.5 128.8 %copy-start.50 = (f32[512]{0:T(512)}, f32[512]{0:T(512)S(1)}, u32[]{:S(2)}) copy-start(f32[512]{0:T(512)S(1)} %fusion.116) | copy-start | bytes 6148
  407.4 100.6 %all-reduce.19.cloned.1.call-start = ((), (), s32[]{:S(2)}) async-start(), calls=%async_computation.9 | async-start | bytes 2359296 | tf_op jit(solution)/shard_map/psum | solution.py:176
  443.7 5.1 copy-start.7
  445.4 14.8 %copy-start.55 = (f32[512]{0:T(512)}, f32[512]{0:T(512)S(1)}, u32[]{:S(2)}) copy-start(f32[512]{0:T(512)S(1)} %fusion.117) | copy-start | bytes 6148
  445.4 16.6 %slice-start = ((s8[8257536]{0:T(1024)(128)(4,1)}), s8[4194304]{0:T(1024)(128)(4,1)S(1)}, s32[]{:S(2)}) async-start(s8[8257536]{0:T(1024)(128)(4,1)} %bitcast.248), calls=%async_computation.16 | async-start | bytes 8388608
  448.8 11.4 copy-start.82
  448.8 13.2 slice-start.1
  470.1 114.4 %all-reduce.23.cloned.1.call-start = ((), (), s32[]{:S(2)}) async-start(), calls=%async_computation.15 | async-start | bytes 3407872 | tf_op jit(solution)/shard_map/psum | solution.py:237
  523.7 15.5 %collective-permute-start.2 = (bf16[512,512]{0,1:T(8,128)(2,1)S(1)}, bf16[512,512]{0,1:T(8,128)(2,1)S(1)}, u32[]{:S(2)}, u32[]{:S(2)}) collective-permute-start(bf16[512,512]{0,1:T(8,128)(2,1)S(1)} %fusion.62), channel_id=1, source_target_pairs={{4,0},{8,4},{12,8},{5,1},{9,5},{13,9},{6,2},{10,6},{14,10},{7,3},{... | collective-permute-start | bytes 1572872 | tf_op jit(solution)/shard_map/ppermute | solution.py:16
  526.0 13.2 copy-start.27
  527.6 12.6 copy-start.65
  527.6 23.5 %copy-start.16 = (bf16[512,1152]{1,0:T(8,128)(2,1)S(1)}, bf16[512,1152]{1,0:T(8,128)(2,1)}, u32[]{:S(2)}) copy-start(bf16[512,1152]{1,0:T(8,128)(2,1)} %copy-done.15) | copy-start | bytes 3538948
  540.1 13.2 copy-start.9
  540.2 117.6 %reduce-scatter.15.cloned.1.call-start = ((), (), s32[]{:S(2)}) async-start(), calls=%async_computation.13 | async-start | bytes 73728
  553.4 32.4 %copy-start.80 = (f32[128]{0:T(128)S(1)}, f32[128]{0:T(128)}, u32[]{:S(2)}) copy-start(f32[128]{0:T(128)} %copy-done.78) | copy-start | bytes 1540
  553.4 33.6 %copy-start.13 = (f32[512,512]{0,1:T(8,128)S(1)}, f32[512,512]{0,1:T(8,128)}, u32[]{:S(2)}) copy-start(f32[512,512]{0,1:T(8,128)} %copy-done.12) | copy-start | bytes 3145732
  553.4 33.6 %copy-start.44 = (f32[512]{0:T(512)S(1)}, f32[512]{0:T(512)}, u32[]{:S(2)}) copy-start(f32[512]{0:T(512)} %copy-done.43) | copy-start | bytes 6148
  553.4 33.6 %copy-start.67 = (f32[1,256]{1,0:T(1,128)S(1)}, f32[1,256]{1,0:T(1,128)}, u32[]{:S(2)}) copy-start(f32[1,256]{1,0:T(1,128)} %copy-done.66) | copy-start | bytes 3076
  555.9 31.2 %copy-start.60 = (f32[512]{0:T(512)S(1)}, f32[512]{0:T(512)}, u32[]{:S(2)}) copy-start(f32[512]{0:T(512)} %copy-done.59) | copy-start | bytes 6148
  585.8 5.0 copy-start.33
  587.4 6.0 copy-start.61
  587.5 9.0 copy-start.23
  587.5 9.0 copy-start.29
  593.4 124.7 %reduce-scatter.13.cloned.1.call-start = ((), (), s32[]{:S(2)}) async-start(), calls=%async_computation.12 | async-start | bytes 331776
  596.4 188.5 %reduce-scatter.9.cloned.1.call-start = ((), (), s32[]{:S(2)}) async-start(), calls=%async_computation.10 | async-start | bytes 1327104 | tf_op jit(solution)/shard_map/reduce_scatter | solution.py:252
  597.7 254.3 %reduce-scatter.11.cloned.1.call-start = ((), (), s32[]{:S(2)}) async-start(), calls=%async_computation.11 | async-start | bytes 1327104 | tf_op jit(solution)/shard_map/reduce_scatter | solution.py:270
  601.1 6.6 copy-start.4
  601.1 755.9 %all-reduce.21.cloned.1.call-start = ((), (), s32[]{:S(2)}) async-start(), calls=%async_computation.14 | async-start | bytes 33030144
  601.1 6.6 copy-start.52
  (55 other events, 137.6 us)
Sparse Core Ops, SparseCore 0:
  10.1 43.7 all-gather.5
  145.8 57.4 all-reduce.14
  206.1 122.8 all-gather.7
  331.0 70.0 all-gather.9
  407.5 36.1 all-reduce.16
  470.2 37.7 all-reduce.18
  540.3 44.1 all-reduce.22
  593.5 62.4 reduce-scatter.14
  659.9 58.1 reduce-scatter.12
  721.3 63.5 reduce-scatter.8
  788.3 63.5 reduce-scatter.10
  855.9 501.0 all-reduce.20
where the time goes:
time: 1380 us; the launch traced here: 1370 us
  waiting for transfers between devices  1040 us (75%)
  blocking collectives  118 us (9%)
  matrix products  74.4 us (5%)
  other arithmetic  55 us (4%)
  local copies, waits for them, and re-layouts  54.8 us (4%)
  between operations  16.5 us (1%)
    unnamed x15, waiting for transfers between devices  564 us
    all_gather x1, waiting for transfers between devices, shards(): lax.all_gather(w_gateup, ('fsdp', 'context'), axis=0, tiled=True)  121 us
    reduce_scatter x1, waiting for transfers between devices, shards(): lax.psum_scatter(jnp.stack([contract_first(features, d_query_low), contra...  65.4 us
    reduce_scatter x1, waiting for transfers between devices, shards(): lax.psum_scatter(keyval_term.astype(jnp.bfloat16), ('fsdp', 'context'), s...  65.4 us
    all_gather x1, waiting for transfers between devices, shards(): lax.all_gather(w_down, ('fsdp', 'context'), axis=0, tiled=True)  58.4 us
    psum x1, waiting for transfers between devices, shards(): branch = lax.psum(contract_last(mixed_low, out_all), 'tensor')  55.3 us
    psum x1, waiting for transfers between devices, shards(): lax.psum(d_normed_part.astype(jnp.bfloat16), 'tensor').astype(jnp.float32)  36.3 us
    psum x1, waiting for transfers between devices, shards(): lax.psum(contract_last(active, lax.all_gather(w_down, ('fsdp', 'context')...  36.1 us
  transfers between devices with their start and end apart: 15, of which 11 were waited for; matrix products, arithmetic and copies ran while one was open for 8% of the time, Pallas kernels for 0%

commit v1 on v0

--- a/solution.py
+++ b/solution.py
@@ -135,7 +135,7 @@
 
     mixed_blocks, log_blocks = lax.map(forward_block, block_starts)
     mixed_low = mixed_blocks.reshape(tokens, local_heads * HD)
-    branch = lax.psum(contract_last(mixed_low, out_all), "tensor")
+    branch = lax.psum(contract_last(mixed_low, out_all).astype(jnp.bfloat16), "tensor").astype(jnp.float32)
     post_attn, post_attn_back = jax.vjp(rms_norm, branch, gains_f[1])
     hidden = inputs + post_attn
     normed_mlp_f, pre_mlp_back = jax.vjp(rms_norm, hidden, gains_f[2])
@@ -182,12 +182,12 @@
         "bn,bkf->nkf", features, d_gate_up, preferred_element_type=jnp.float32
     )
     down_term = contract_first(grad_cols, active)
-    mlp_grads = lax.psum_scatter(
-        jnp.concatenate([gate_up_term, down_term[:, None, :]], axis=1).astype(jnp.bfloat16),
-        ("fsdp", "context"),
-        scatter_dimension=0,
-        tiled=True,
+    scatter = lambda part: lax.psum_scatter(
+        part.astype(jnp.bfloat16), ("fsdp", "context"), scatter_dimension=0, tiled=True
     ).astype(jnp.float32)
+    gate_grad = scatter(gate_up_term[:, 0])
+    up_grad = scatter(gate_up_term[:, 1])
+    down_grad = scatter(down_term)
     d_branch, gain_post_attn = post_attn_back(d_hidden)
     branch_low = d_branch.astype(jnp.bfloat16)
     d_mixed = jnp.dot(branch_low, out_all, preferred_element_type=jnp.float32)
@@ -279,8 +279,8 @@
         attn_grads[:, 0],
         keyval_weight_grad,
         attn_grads[:, 1],
-        mlp_grads[:, :2],
-        mlp_grads[:, 2],
+        jnp.stack([gate_grad, up_grad], axis=1),
+        down_grad,
     )
 
 

time: 1380 us -> 1120 us (0.81)
  waiting for transfers between devices: 1040 us -> 796 us
    unnamed x15 -> x18, waiting for transfers between devices: 564 us -> 256 us
    reduce_scatter x0 -> x1, waiting for transfers between devices: none -> 83.7 us  [shards(): lax.psum_scatter(part.astype(jnp.bfloat16), ('fsdp', 'context'), scatter_...]
    concatenate x1 -> x0, local copies, waits for them, and re-layouts: 27.1 us -> none  [shards(): jnp.concatenate([gate_up_term, down_term[:, None, :]], axis=1)]
    unnamed x183 -> x180, local copies, waits for them, and re-layouts: 18.7 us -> 39.6 us
    psum x1, waiting for transfers between devices: 55.3 us -> 35.9 us  [shards(): lax.psum(contract_last(mixed_low, out_all).astype(jnp.bfloat16), 'tensor')]
  transfers between devices with their start and end apart: 15 -> 17, of which waited for: 11 -> 14; matrix products, arithmetic and copies ran while one was open for 8% -> 9% of each run, Pallas kernels for 0% -> 0%
where the time goes in v1:
time: 1120 us; the launch traced here: 1110 us
  waiting for transfers between devices  796 us (71%)
  blocking collectives  120 us (11%)
  matrix products  72.4 us (6%)
  local copies, waits for them, and re-layouts  50.5 us (5%)
  other arithmetic  49.1 us (4%)
  between operations  15.3 us (1%)
    unnamed x18, waiting for transfers between devices  256 us
    all_gather x1, waiting for transfers between devices, shards(): lax.all_gather(w_gateup, ('fsdp', 'context'), axis=0, tiled=True)  119 us
    reduce_scatter x1, waiting for transfers between devices, shards(): lax.psum_scatter(part.astype(jnp.bfloat16), ('fsdp', 'context'), scatter_...  83.7 us
    reduce_scatter x1, waiting for transfers between devices, shards(): lax.psum_scatter(jnp.stack([contract_first(features, d_query_low), contra...  65.7 us
    reduce_scatter x1, waiting for transfers between devices, shards(): lax.psum_scatter(keyval_term.astype(jnp.bfloat16), ('fsdp', 'context'), s...  65.5 us
    all_gather x1, waiting for transfers between devices, shards(): lax.all_gather(w_down, ('fsdp', 'context'), axis=0, tiled=True)  58.5 us
    unnamed x180, local copies, waits for them, and re-layouts  39.6 us
    psum x1, waiting for transfers between devices, shards(): lax.psum(d_normed_part.astype(jnp.bfloat16), 'tensor').astype(jnp.float32)  36.4 us
  transfers between devices with their start and end apart: 17, of which 14 were waited for; matrix products, arithmetic and copies ran while one was open for 9% of the time, Pallas kernels for 0%

profile of v1, /device:TPU:0, one launch (start us, length us, event | category | flops | bytes accessed | tf_op | source)
XLA Modules:
  0.0 1111.9 jit_solution(1959116816128827641)
XLA Ops:
  8.7 4.9 collective-permute-start.1
  14.3 18.8 %all-gather.1 = bf16[8,32,2]{1,2,0:T(2,128)(2,1)S(1)} all-gather(bf16[1,32,2]{1,2,0:T(2,128)(2,1)} %bitcast.266), channel_id=1, replica_groups=mesh['fsdp'=2,'context'=4,'tensor'=4] {'fsdp','context'}, dimensions={0}, use_global_device_ids=true | all-gather | bytes 1152 | tf_op jit(solution)/shard_map/all_gather | solution.py:75
  33.2 27.2 %all-gather = bf16[8,144,4]{1,2,0:T(4,128)(2,1)S(1)} all-gather(bf16[1,144,4]{1,2,0:T(4,128)(2,1)} %bitcast.265), channel_id=1, replica_groups=mesh['fsdp'=2,'context'=4,'tensor'=4] {'fsdp','context'}, dimensions={0}, use_global_device_ids=true | all-gather | bytes 10368 | tf_op jit(solution)/shard_map/all_gather | solution.py:74
  62.8 32.5 %all_gather.26 = bf16[1152,256]{1,0:T(8,128)(2,1)S(1)} all-gather(bf16[144,256]{1,0:T(8,128)(2,1)} %param.20), channel_id=1, replica_groups=mesh['fsdp'=2,'context'=4,'tensor'=4] {'fsdp','context'}, dimensions={0}, use_global_device_ids=true | all-gather | bytes 663552 | tf_op jit(solution)/shard_map/all_gather | solution.py:76
  96.1 2.0 multiply_reduce_fusion.1
  99.1 2.2 fusion.131
  104.4 33.8 %all_gather.27 = bf16[1152,256]{1,0:T(8,128)(2,1)S(1)} all-gather(bf16[144,256]{1,0:T(8,128)(2,1)S(1)} %copy-done.32), channel_id=1, replica_groups=mesh['fsdp'=2,'context'=4,'tensor'=4] {'fsdp','context'}, dimensions={0}, use_global_device_ids=true | all-gather | bytes 663552 | tf_op jit(solution)/shard_map/all_gather | solution.py:78
  138.4 2.0 fusion.140
  143.1 2.3 copy.32
  146.3 35.9 %all-reduce.13.cloned.1.call-done = bf16[512,1152]{1,0:T(8,128)(2,1)} async-done(((bf16[512,1152]{1,0:T(8,128)(2,1)}), bf16[512,1152]{1,0:T(8,128)(2,1)}) %all-reduce.13.cloned.1.call-update) | async-done | bytes 1179664 | tf_op jit(solution)/shard_map/psum | solution.py:138
  185.0 2.3 multiply_reduce_fusion
  188.5 119.4 %all-gather.8.cloned.1.call-done = bf16[1152,2,1728]{2,0,1:T(8,128)(2,1)} async-done(((bf16[144,2,1728]{2,0,1:T(8,128)(2,1)}), bf16[1152,2,1728]{2,0,1:T(8,128)(2,1)}) %all-gather.8.cloned.1.call-update) | async-done | bytes 7962640 | tf_op jit(solution)/shard_map/all_gather | solution.py:147
  307.9 8.2 fusion.114
  316.1 2.9 copy-done.8
  319.0 2.4 multiply_convert_fusion
  321.4 58.5 %all-gather.10.cloned.1.call-done = bf16[1152,1728]{1,0:T(8,128)(2,1)} async-done(((bf16[144,1728]{1,0:T(8,128)(2,1)}), bf16[1152,1728]{1,0:T(8,128)(2,1)}) %all-gather.10.cloned.1.call-update) | async-done | bytes 3981328 | tf_op jit(solution)/shard_map/all_gather | solution.py:154
  380.0 6.3 convolution_convert_fusion.4
  386.9 35.7 %all-reduce.15.cloned.1.call-done = bf16[512,1152]{1,0:T(8,128)(2,1)} async-done(((bf16[512,1152]{1,0:T(8,128)(2,1)}), bf16[512,1152]{1,0:T(8,128)(2,1)}) %all-reduce.15.cloned.1.call-update) | async-done | bytes 1179664 | tf_op jit(solution)/shard_map/psum | solution.py:152
  424.3 3.4 fusion.38
  427.8 10.7 multiply_bitcast_fusion
  440.2 8.1 fusion.7
  449.9 36.4 %all-reduce.17.cloned.1.call-done = bf16[512,1152]{1,0:T(8,128)(2,1)} async-done(((bf16[512,1152]{1,0:T(8,128)(2,1)}), bf16[512,1152]{1,0:T(8,128)(2,1)}) %all-reduce.17.cloned.1.call-update) | async-done | bytes 1179664 | tf_op jit(solution)/shard_map/psum | solution.py:176
  486.3 3.6 fusion.29
  490.0 5.1 fusion.25
  505.6 11.6 %collective-permute-done.2 = bf16[512,512]{0,1:T(8,128)(2,1)S(1)} collective-permute-done((bf16[512,512]{0,1:T(8,128)(2,1)S(1)}, bf16[512,512]{0,1:T(8,128)(2,1)S(1)}, u32[]{:S(2)}, u32[]{:S(2)}) %collective-permute-start.2) | collective-permute-done | bytes 524320 | tf_op jit(solution)/shard_map/ppermute | solution.py:16
  523.4 7.2 psum.47
  530.6 2.3 fusion.22
  532.9 2.5 fusion.21
  535.5 27.2 %all-reduce.19.cloned.1.call-done = (bf16[512,1152]{1,0:T(8,128)(2,1)}, bf16[512,512]{0,1:T(8,128)(2,1)}) async-done(((bf16[512,1152]{1,0:T(8,128)(2,1)}, bf16[512,512]{0,1:T(8,128)(2,1)}), (bf16[512,1152]{1,0:T(8,128)(2,1)}, bf16[512,512]{0,1:T(8,128)(2,1)})) %all-reduce.19.cloned.1.call-update) | async-done | bytes 1703952 | tf_op jit(solution)/shard_map/psum | solution.py:237
  565.6 3.2 fusion.27
  576.1 3.1 convolution_convert_fusion.2
  579.2 9.3 convolution_convert_fusion
  588.6 3.5 slice_bitcast_fusion.1
  592.1 6.5 copy.38
  598.6 6.5 copy.40
  606.7 6.3 convolution_convert_fusion.1
  613.7 4.0 fusion.52
  617.8 16.4 %reduce-scatter.24.cloned.1.call-done = bf16[32,2]{1,0:T(8,128)(2,1)} async-done(((bf16[256,2]{1,0:T(8,128)(2,1)}), bf16[32,2]{1,0:T(8,128)(2,1)}) %reduce-scatter.24.cloned.1.call-update) | async-done | bytes 144
  635.5 60.7 %reduce-scatter.22.cloned.1.call-done = bf16[144,4]{1,0:T(8,128)(2,1)} async-done(((bf16[1152,4]{1,0:T(8,128)(2,1)}), bf16[144,4]{1,0:T(8,128)(2,1)}) %reduce-scatter.22.cloned.1.call-update) | async-done | bytes 1168
  697.7 65.7 %reduce-scatter.16.cloned.1.call-done = bf16[144,2,256]{2,0,1:T(8,128)(2,1)} async-done(((bf16[1152,2,256]{2,0,1:T(8,128)(2,1)}), bf16[144,2,256]{2,0,1:T(8,128)(2,1)}) %reduce-scatter.16.cloned.1.call-update) | async-done | bytes 147472 | tf_op jit(solution)/shard_map/reduce_scatter | solution.py:252
  765.0 65.5 %reduce-scatter.18.cloned.1.call-done = bf16[144,512]{1,0:T(8,128)(2,1)} async-done(((bf16[1152,512]{1,0:T(8,128)(2,1)}), bf16[144,512]{1,0:T(8,128)(2,1)}) %reduce-scatter.18.cloned.1.call-update) | async-done | bytes 147472 | tf_op jit(solution)/shard_map/reduce_scatter | solution.py:270
  832.2 88.8 %reduce-scatter.26.cloned.1.call-done = bf16[144,1728]{1,0:T(8,128)(2,1)} async-done(((bf16[1152,1728]{1,0:T(8,128)(2,1)}), bf16[144,1728]{1,0:T(8,128)(2,1)}) %reduce-scatter.26.cloned.1.call-update) | async-done | bytes 497680
  921.0 2.3 copy.39
  923.2 88.9 %reduce-scatter.28.cloned.1.call-done = bf16[144,1728]{1,0:T(8,128)(2,1)} async-done(((bf16[1152,1728]{1,0:T(8,128)(2,1)}), bf16[144,1728]{1,0:T(8,128)(2,1)}) %reduce-scatter.28.cloned.1.call-update) | async-done | bytes 497680
  1012.1 2.3 copy.41
  1016.2 3.2 copy.33
  1019.4 83.7 %reduce-scatter.20.cloned.1.call-done = bf16[144,1728]{1,0:T(8,128)(2,1)} async-done(((bf16[1152,1728]{1,0:T(8,128)(2,1)}), bf16[144,1728]{1,0:T(8,128)(2,1)}) %reduce-scatter.20.cloned.1.call-update) | async-done | bytes 497680 | tf_op jit(solution)/shard_map/reduce_scatter | solution.py:185
  1103.1 2.1 convert_element_type.221
  (279 shorter events, 59.4 us)
Async XLA Ops:
  7.2 91.9 %all-gather.6.cloned.1.call-start = ((), (), s32[]{:S(2)}) async-start(), calls=%async_computation.7 | async-start | bytes 1327104 | tf_op jit(solution)/shard_map/all_gather | solution.py:77
  7.9 174.3 %all-reduce.13.cloned.1.call-start = ((), (), s32[]{:S(2)}) async-start(), calls=%async_computation.8 | async-start | bytes 2359296 | tf_op jit(solution)/shard_map/psum | solution.py:138
  8.7 129.6 %collective-permute-start.1 = (s32[2,512]{1,0:T(2,128)S(1)}, s32[2,512]{1,0:T(2,128)S(1)}, u32[]{:S(2)}, u32[]{:S(2)}) collective-permute-start(s32[2,512]{1,0:T(2,128)S(1)} %pad_add_fusion.2), channel_id=1, source_target_pairs={{0,4},{4,8},{8,12},{1,5},{5,9},{9,13},{2,6},{6,10},{10,14},{3,7},{... | collective-permute-start | bytes 12296 | tf_op jit(solution)/shard_map/ppermute | solution.py:16
  14.3 87.4 %copy-start.37 = (f32[512]{0:T(512)}, f32[512]{0:T(512)S(1)}, u32[]{:S(2)}) copy-start(f32[512]{0:T(512)S(1)} %convert_element_type.178) | copy-start | bytes 6148
  60.5 41.2 %copy-start.73 = (f32[128]{0:T(128)}, f32[128]{0:T(128)S(1)}, u32[]{:S(2)}) copy-start(f32[128]{0:T(128)S(1)} %multiply_power_fusion) | copy-start | bytes 1540
  61.1 38.0 %copy-start.44 = (f32[1152]{0:T(1024)}, f32[1152]{0:T(1024)S(1)}, u32[]{:S(2)}) copy-start(f32[1152]{0:T(1024)S(1)} %get-tuple-element.146) | copy-start | bytes 13828
  62.7 36.3 %copy-start.52 = (f32[512]{0:T(512)}, f32[512]{0:T(512)S(1)}, u32[]{:S(2)}) copy-start(f32[512]{0:T(512)S(1)} %fusion.30) | copy-start | bytes 6148
  62.7 36.4 %copy-start.70 = (f32[512]{0:T(512)}, f32[512]{0:T(512)S(1)}, u32[]{:S(2)}) copy-start(f32[512]{0:T(512)S(1)} %fusion.116) | copy-start | bytes 6148
  62.7 36.3 %copy-start.63 = (f32[1,256]{1,0:T(1,128)}, f32[1,256]{1,0:T(1,128)S(1)}, u32[]{:S(2)}) copy-start(f32[1,256]{1,0:T(1,128)S(1)} %get-tuple-element.171) | copy-start | bytes 3076
  62.8 38.8 %copy-start.61 = (f32[1,256]{1,0:T(1,128)}, f32[1,256]{1,0:T(1,128)S(1)}, u32[]{:S(2)}) copy-start(f32[1,256]{1,0:T(1,128)S(1)} %get-tuple-element.172) | copy-start | bytes 3076
  62.8 36.3 %copy-start.1 = (bf16[1,512,1152]{2,1,0:T(8,128)(2,1)S(1)}, bf16[1,512,1152]{2,1,0:T(8,128)(2,1)}, u32[]{:S(2)}) copy-start(bf16[1,512,1152]{2,1,0:T(8,128)(2,1)} %param.15) | copy-start | bytes 3538948
  101.5 36.7 %copy-start.60 = (s32[1,512]{1,0:T(1,128)S(1)}, s32[1,512]{1,0:T(1,128)}, u32[]{:S(2)}) copy-start(s32[1,512]{1,0:T(1,128)} %param.16) | copy-start | bytes 6148
  101.6 36.7 %copy-start.67 = (s32[1,512]{1,0:T(1,128)S(1)}, s32[1,512]{1,0:T(1,128)}, u32[]{:S(2)}) copy-start(s32[1,512]{1,0:T(1,128)} %param.17) | copy-start | bytes 6148
  103.0 35.3 %collective-permute-start = (bf16[512,512]{0,1:T(8,128)(2,1)S(1)}, bf16[512,512]{0,1:T(8,128)(2,1)S(1)}, u32[]{:S(2)}, u32[]{:S(2)}) collective-permute-start(bf16[512,512]{0,1:T(8,128)(2,1)S(1)} %pad_maximum_fusion.2), channel_id=1, source_target_pairs={{0,4},{4,8},{8,12},{1,5},{5,9},{9,13},{2,6},{6,10},{10,14},{3,7},{... | collective-permute-start | bytes 1572872 | tf_op jit(solution)/shard_map/ppermute | solution.py:16
  141.4 3.9 copy-start.26
  143.0 164.9 %all-gather.8.cloned.1.call-start = ((), (), s32[]{:S(2)}) async-start(), calls=%async_computation.9 | async-start | bytes 9289728 | tf_op jit(solution)/shard_map/all_gather | solution.py:147
  145.4 234.6 %all-gather.10.cloned.1.call-start = ((), (), s32[]{:S(2)}) async-start(), calls=%async_computation.10 | async-start | bytes 4644864 | tf_op jit(solution)/shard_map/all_gather | solution.py:154
  146.0 276.6 %all-reduce.15.cloned.1.call-start = ((), (), s32[]{:S(2)}) async-start(), calls=%async_computation.11 | async-start | bytes 2359296 | tf_op jit(solution)/shard_map/psum | solution.py:152
  182.2 125.7 %copy-start = (bf16[512,1152]{1,0:T(8,128)(2,1)S(1)}, bf16[512,1152]{1,0:T(8,128)(2,1)}, u32[]{:S(2)}) copy-start(bf16[512,1152]{1,0:T(8,128)(2,1)} %all-reduce.13.cloned.1.call-done) | copy-start | bytes 3538948
  386.3 100.0 %all-reduce.17.cloned.1.call-start = ((), (), s32[]{:S(2)}) async-start(), calls=%async_computation.12 | async-start | bytes 2359296 | tf_op jit(solution)/shard_map/psum | solution.py:176
  422.6 5.2 copy-start.5
  422.6 5.2 copy-start.12
  424.3 14.2 %copy-start.47 = (f32[512]{0:T(512)}, f32[512]{0:T(512)S(1)}, u32[]{:S(2)}) copy-start(f32[512]{0:T(512)S(1)} %fusion.121) | copy-start | bytes 6148
  424.3 15.9 %slice-start = ((s8[8257536]{0:T(1024)(128)(4,1)}), s8[4194304]{0:T(1024)(128)(4,1)S(1)}, s32[]{:S(2)}) async-start(s8[8257536]{0:T(1024)(128)(4,1)} %bitcast.267), calls=%async_computation.21 | async-start | bytes 8388608
  427.8 10.7 copy-start.77
  427.8 12.5 %slice-start.1 = ((s8[8257536]{0:T(1024)(128)(4,1)}), s8[4063232]{0:T(1024)(128)(4,1)S(1)}, s32[]{:S(2)}) async-start(s8[8257536]{0:T(1024)(128)(4,1)} %bitcast.267), calls=%async_computation.22 | async-start | bytes 8126464
  448.4 114.3 %all-reduce.19.cloned.1.call-start = ((), (), s32[]{:S(2)}) async-start(), calls=%async_computation.20 | async-start | bytes 3407872 | tf_op jit(solution)/shard_map/psum | solution.py:237
  490.0 5.1 copy-start.57
  501.7 15.5 %collective-permute-start.2 = (bf16[512,512]{0,1:T(8,128)(2,1)S(1)}, bf16[512,512]{0,1:T(8,128)(2,1)S(1)}, u32[]{:S(2)}, u32[]{:S(2)}) collective-permute-start(bf16[512,512]{0,1:T(8,128)(2,1)S(1)} %fusion.66), channel_id=1, source_target_pairs={{4,0},{8,4},{12,8},{5,1},{9,5},{13,9},{6,2},{10,6},{14,10},{7,3},{... | collective-permute-start | bytes 1572872 | tf_op jit(solution)/shard_map/ppermute | solution.py:16
  504.1 13.2 %copy-start.25 = (bf16[512,256]{0,1:T(8,128)(2,1)}, bf16[512,256]{0,1:T(8,128)(2,1)S(1)}, u32[]{:S(2)}) copy-start(bf16[512,256]{0,1:T(8,128)(2,1)S(1)} %fusion.108) | copy-start | bytes 786436
  505.6 25.0 %copy-start.17 = (bf16[512,1152]{1,0:T(8,128)(2,1)S(1)}, bf16[512,1152]{1,0:T(8,128)(2,1)}, u32[]{:S(2)}) copy-start(bf16[512,1152]{1,0:T(8,128)(2,1)} %copy-done.16) | copy-start | bytes 3538948
  518.2 14.7 %copy-start.3 = (bf16[1,512,1152]{2,1,0:T(8,128)(2,1)S(1)}, bf16[1,512,1152]{2,1,0:T(8,128)(2,1)}, u32[]{:S(2)}) copy-start(bf16[1,512,1152]{2,1,0:T(8,128)(2,1)} %param.15) | copy-start | bytes 3538948
  518.2 115.9 %reduce-scatter.24.cloned.1.call-start = ((), (), s32[]{:S(2)}) async-start(), calls=%async_computation.17 | async-start | bytes 73728
  532.9 31.0 %copy-start.39 = (f32[512]{0:T(512)S(1)}, f32[512]{0:T(512)}, u32[]{:S(2)}) copy-start(f32[512]{0:T(512)} %copy-done.37) | copy-start | bytes 6148
  532.9 31.0 %copy-start.75 = (f32[128]{0:T(128)S(1)}, f32[128]{0:T(128)}, u32[]{:S(2)}) copy-start(f32[128]{0:T(128)} %copy-done.73) | copy-start | bytes 1540
  532.9 32.2 %copy-start.10 = (f32[512,512]{0,1:T(8,128)S(1)}, f32[512,512]{0,1:T(8,128)}, u32[]{:S(2)}) copy-start(f32[512,512]{0,1:T(8,128)} %copy-done.9) | copy-start | bytes 3145732
  532.9 32.2 %copy-start.41 = (f32[512]{0:T(512)S(1)}, f32[512]{0:T(512)}, u32[]{:S(2)}) copy-start(f32[512]{0:T(512)} %copy-done.40) | copy-start | bytes 6148
  532.9 32.2 %copy-start.62 = (f32[1,256]{1,0:T(1,128)S(1)}, f32[1,256]{1,0:T(1,128)}, u32[]{:S(2)}) copy-start(f32[1,256]{1,0:T(1,128)} %copy-done.61) | copy-start | bytes 3076
  535.5 29.9 %copy-start.55 = (f32[512]{0:T(512)S(1)}, f32[512]{0:T(512)}, u32[]{:S(2)}) copy-start(f32[512]{0:T(512)} %copy-done.54) | copy-start | bytes 6148
  563.9 4.9 copy-start.28
  565.6 9.0 copy-start.22
  565.6 9.0 copy-start.27
  571.5 124.7 %reduce-scatter.22.cloned.1.call-start = ((), (), s32[]{:S(2)}) async-start(), calls=%async_computation.16 | async-start | bytes 331776
  574.5 188.8 %reduce-scatter.16.cloned.1.call-start = ((), (), s32[]{:S(2)}) async-start(), calls=%async_computation.13 | async-start | bytes 1327104 | tf_op jit(solution)/shard_map/reduce_scatter | solution.py:252
  575.8 254.7 %reduce-scatter.18.cloned.1.call-start = ((), (), s32[]{:S(2)}) async-start(), calls=%async_computation.14 | async-start | bytes 1327104 | tf_op jit(solution)/shard_map/reduce_scatter | solution.py:270
  579.2 341.8 %reduce-scatter.26.cloned.1.call-start = ((), (), s32[]{:S(2)}) async-start(), calls=%async_computation.18 | async-start | bytes 4644864
  598.5 413.5 %reduce-scatter.28.cloned.1.call-start = ((), (), s32[]{:S(2)}) async-start(), calls=%async_computation.19 | async-start | bytes 4644864
  605.1 498.0 %reduce-scatter.20.cloned.1.call-start = ((), (), s32[]{:S(2)}) async-start(), calls=%async_computation.15 | async-start | bytes 4644864 | tf_op jit(solution)/shard_map/reduce_scatter | solution.py:185
  (54 other events, 118.6 us)
Sparse Core Ops, SparseCore 0:
  10.1 43.7 all-gather.5
  143.1 38.9 all-reduce.12
  184.9 122.9 all-gather.7
  309.9 70.0 all-gather.9
  386.4 36.1 all-reduce.14
  448.5 37.7 all-reduce.16
  518.4 44.2 all-reduce.18
  571.6 62.4 reduce-scatter.23
  638.0 58.1 reduce-scatter.21
  699.4 63.8 reduce-scatter.15
  766.8 63.7 reduce-scatter.17
  834.0 86.9 reduce-scatter.25
  924.5 87.5 reduce-scatter.27
  1015.5 87.5 reduce-scatter.19

commit v2 on v1

--- a/solution.py
+++ b/solution.py
@@ -1,6 +1,10 @@
+import functools
+
 import jax
 import jax.numpy as jnp
 from jax import lax
+from jax.experimental import pallas as pl
+from jax.experimental.pallas import tpu as pltpu
 from jax.sharding import PartitionSpec as P
 
 HD = 256
@@ -50,6 +54,884 @@
     return lax.dot_general(
         left_side, right_side, (((0,), (0,)), ((), ())), preferred_element_type=jnp.float32
     )
+
+
+MESH = pl.DeviceIdType.MESH
+F32 = jnp.float32
+BF16 = jnp.bfloat16
+LANES = 128
+SEMAPHORES = 112
+
+
+def mm(left, right):
+    return jnp.dot(left, right, preferred_element_type=F32)
+
+
+def rms_factor(values):
+    return lax.rsqrt(jnp.mean(values * values, axis=-1, keepdims=True) + EPSILON)
+
+
+def rms_backward(grad, values, factor, gain):
+    unit = values * factor
+    scaled = grad * gain
+    inner = jnp.mean(scaled * unit, axis=-1, keepdims=True)
+    return factor * (scaled - unit * inner), jnp.sum(grad * unit, axis=0, keepdims=True)
+
+
+def turn(values, cosine, sine):
+    half = values.shape[-1] // 2
+    first, second = values[:, :half], values[:, half:]
+    return jnp.concatenate([first * cosine - second * sine, second * cosine + first * sine], axis=1)
+
+
+def turn_back(values, cosine, sine):
+    half = values.shape[-1] // 2
+    first, second = values[:, :half], values[:, half:]
+    return jnp.concatenate([first * cosine + second * sine, second * cosine - first * sine], axis=1)
+
+
+def fused_kernel(
+    sizes,
+    act,
+    cosine,
+    sine,
+    seg_row,
+    seg_col,
+    cot_all,
+    w_attn,
+    w_ff,
+    out_block,
+    out_input,
+    out_gains,
+    out_ff,
+    out_attn,
+    out_kv,
+    cot,
+    wa,
+    wf,
+    seg_left,
+    gain_rows,
+    head_rows,
+    nrm,
+    qraw,
+    kraw,
+    qs,
+    kv,
+    probs,
+    mix,
+    p4,
+    p4_core,
+    p4_sum,
+    p4_chip,
+    hid,
+    bran,
+    xg,
+    gel,
+    upg,
+    active,
+    p8,
+    p8_core,
+    p8_sum,
+    p8_chip,
+    dd,
+    dhid,
+    db,
+    dscore,
+    dmix,
+    dq,
+    kvp,
+    kvp_core,
+    kvp_sum,
+    kvp_chip,
+    ret_out,
+    ret_in,
+    dkv,
+    gall_x,
+    gall_z,
+    ga,
+    ga_x,
+    ga_z,
+    kvg,
+    ff_stage,
+    gain_mine,
+    gain_tensor,
+    gain_x,
+    gain_z,
+    block_all,
+    input_all,
+    ss,
+    rs,
+    ls,
+):
+    C = sizes["context"]
+    T, D, R, U = sizes["tokens"], sizes["width"], sizes["rows"], sizes["units"]
+    S = T // 4
+    f = lax.axis_index("fsdp")
+    c = lax.axis_index("context")
+    t = lax.axis_index("tensor")
+    y, core = t // 2, t % 2
+    m = c % 2
+    base = c - m
+    partner = {"tensor": y * 2 + (1 - core)}
+    across = {"fsdp": 1 - f}
+    counter = [0]
+    sent = []
+
+    def slots(count):
+        first = counter[0]
+        counter[0] += count
+        assert counter[0] <= SEMAPHORES
+        return first
+
+    def copy(k, src, dst, device):
+        return pltpu.make_async_remote_copy(
+            src_ref=src,
+            dst_ref=dst,
+            send_sem=ss.at[k],
+            recv_sem=rs.at[k],
+            device_id=device,
+            device_id_type=MESH,
+        )
+
+    def send(k, src, dst, device):
+        moved = copy(k, src, dst, device)
+        moved.start()
+        sent.append(moved)
+
+    def arrive(k, dst):
+        copy(k, dst, dst, partner).wait_recv()
+
+    def settle():
+        for moved in sent:
+            moved.wait_send()
+        sent.clear()
+
+    def along(step):
+        return {"context": (c + step) % C}
+
+    def rows_of(ff, cc):
+        return pl.ds(pl.multiple_of((ff * C + cc) * R, R), R)
+
+    def chip_of(k, count):
+        if count == 2:
+            return {"tensor": k * 2 + core}
+        return {"context": base + k // 2, "tensor": (k % 2) * 2 + core}
+
+    barrier = pltpu.get_barrier_semaphore()
+    greeted = [along(step) for step in range(1, C)] + [across]
+    greeted += [{"tensor": (t + step) % 4} for step in range(1, 4)]
+    greeted += [{"context": base + 1 - m, "tensor": (1 - y) * 2 + core}]
+    for device in greeted:
+        pl.semaphore_signal(barrier, inc=1, device_id=device, device_id_type=MESH)
+    pl.semaphore_wait(barrier, len(greeted))
+
+    mine = rows_of(f, c)
+    own_attn = pltpu.make_async_copy(w_attn, wa.at[mine], ls.at[0])
+    own_attn.start()
+    ka = slots(2 * C)
+    for step in range(1, C):
+        send(ka + step, w_attn, wa.at[mine], along(step))
+    send(ka, w_attn, wa.at[mine], across)
+    ks = slots(1)
+
+    @pl.when(c < C - 1)
+    def _():
+        copy(ks, seg_row, seg_left, {"context": c + 1}).start()
+
+    shard = pl.ds(pl.multiple_of(t * S, S), S)
+    own_cot = pltpu.make_async_copy(cot_all.at[shard], cot, ls.at[2])
+    own_cot.start()
+    own_ff = pltpu.make_async_copy(w_ff.at[m], wf.at[:, mine], ls.at[1])
+    own_ff.start()
+    own_attn.wait()
+    for step in range(1, C):
+        block = wa.at[rows_of(f, (c - step + C) % C)]
+        arrive(ka + step, block)
+        send(ka + C + step, block, block, across)
+    arrive(ka, wa.at[rows_of(1 - f, c)])
+    for step in range(1, C):
+        arrive(ka + C + step, wa.at[rows_of(1 - f, (c - step + C) % C)])
+
+    @pl.when(c > 0)
+    def _():
+        arrive(ks, seg_left)
+
+    @pl.when(c == 0)
+    def _():
+        seg_left[...] = jnp.full(seg_left.shape, -1, jnp.int32)
+        kv[0:T] = jnp.zeros((T, 2 * HD), BF16)
+
+    gain_t = jnp.transpose(wa[:, 4 * HD :].astype(F32))
+    gain_rows[...] = gain_t[0:8]
+    narrow = HD // (2 * C)
+    here = lax.broadcasted_iota(jnp.int32, (D, HD), 0)
+    want = lax.broadcasted_iota(jnp.int32, (D, HD), 1)
+    shift = narrow.bit_length() - 1
+    want = lax.shift_right_logical(want, shift) * R + (want & (narrow - 1))
+    pick = jnp.where(here == want, 1.0, 0.0).astype(BF16)
+    head_rows[...] = mm(gain_t[0:16].astype(BF16), pick)[0:8]
+
+    def gain(index):
+        return gain_rows[index : index + 1]
+
+    def head_gain(index):
+        return head_rows[4 + index : 5 + index]
+
+    half = T // 2
+
+    def project(i, _):
+        rows = pl.ds(pl.multiple_of(i * half, half), half)
+        values = act[rows].astype(F32)
+        low = (values * rms_factor(values) * gain(0)).astype(BF16)
+        nrm[rows] = low
+        raw_q = mm(low, wa[:, 0:HD])
+        raw_kv = mm(low, wa[:, HD : 3 * HD])
+        raw_k = raw_kv[:, :HD]
+        qraw[rows] = raw_q
+        kraw[rows] = raw_k
+        cos, sin = cosine[rows], sine[rows]
+        qs[rows] = turn(raw_q * rms_factor(raw_q) * head_gain(0), cos, sin).astype(BF16)
+        own = pl.ds(pl.multiple_of(T + i * half, half), half)
+        kv[own, 0:HD] = turn(raw_k * rms_factor(raw_k) * head_gain(1), cos, sin).astype(BF16)
+        kv[own, HD:] = raw_kv[:, HD:].astype(BF16)
+        return 0
+
+    lax.fori_loop(0, 2, project, 0)
+
+    kk = slots(2)
+    my_half = pl.ds(pl.multiple_of(core * half, half), half)
+    other_half = pl.ds(pl.multiple_of((1 - core) * half, half), half)
+    own_half = pl.ds(pl.multiple_of(T + core * half, half), half)
+
+    @pl.when(c < C - 1)
+    def _():
+        copy(kk, kv.at[own_half], kv.at[my_half], {"context": c + 1}).start()
+
+    kf = slots(2 * C)
+    for step in range(1, C):
+        send(kf + step, w_ff.at[(c + step) % 2], wf.at[:, mine], along(step))
+    send(kf, w_ff.at[m], wf.at[:, mine], across)
+
+    @pl.when(c > 0)
+    def _():
+        arrive(kk, kv.at[my_half])
+        moved = copy(kk + 1, kv.at[my_half], kv.at[my_half], partner)
+        moved.start()
+        arrive(kk + 1, kv.at[other_half])
+        moved.wait_send()
+
+    scale = HD**-0.5
+    no_left = jnp.where(c > 0, 0, 2 * T)
+    k4 = slots(2)
+
+    def attend(i, _):
+        rows = pl.ds(pl.multiple_of(i * half, half), half)
+        q = qs[rows]
+        labels = seg_col[rows]
+        row = lax.broadcasted_iota(jnp.int32, (half, T), 0) + i * half
+        col = lax.broadcasted_iota(jnp.int32, (half, T), 1)
+        left = contract_last(q, kv[0:T, 0:HD]) * scale
+        left = jnp.where((labels == seg_left[0:1]) & (col > row + no_left), left, -1e30)
+        own = contract_last(q, kv[T:, 0:HD]) * scale
+        own = jnp.where((labels == seg_row[0:1]) & (col <= row), own, -1e30)
+        top = jnp.maximum(
+            jnp.max(left, axis=1, keepdims=True), jnp.max(own, axis=1, keepdims=True)
+        )
+        left, own = jnp.exp(left - top), jnp.exp(own - top)
+        total = jnp.sum(left, axis=1, keepdims=True) + jnp.sum(own, axis=1, keepdims=True)
+        left, own = left / total, own / total
+        probs[rows, 0:T] = left
+        probs[rows, T:] = own
+        mixed = mm(left.astype(BF16), kv[0:T, HD:]) + mm(own.astype(BF16), kv[T:, HD:])
+        mixed = mixed.astype(BF16)
+        mix[rows] = mixed
+        part = contract_last(mixed, wa[:, 3 * HD : 4 * HD]).astype(BF16)
+        p4[i, 0] = part[0:S]
+        p4[i, 1] = part[S:]
+        copy(k4 + i, p4.at[i, 1 - core], p4_core.at[i], partner).start()
+        return 0
+
+    lax.fori_loop(0, 2, attend, 0)
+
+    def relay_ff(step):
+        block = wf.at[:, rows_of(f, (c - step + C) % C)]
+        arrive(kf + step, block)
+        send(kf + C + step, block, block, across)
+
+    def sum4(k):
+        kc = slots(1)
+        arrive(k + (1 - y), p4_core.at[1 - y])
+        p4_sum[...] = (
+            p4[1 - y, core].astype(F32) + p4_core[1 - y].astype(F32)
+        ).astype(BF16)
+        copy(kc, p4_sum, p4_chip, chip_of(1 - y, 2)).start()
+        arrive(k + y, p4_core.at[y])
+        return kc
+
+    def finish4(kc):
+        arrive(kc, p4_chip)
+        return (
+            p4[y, core].astype(F32)
+            + p4_core[y].astype(F32)
+            + p4_chip[...].astype(F32)
+        )
+
+    kc = sum4(k4)
+    relay_ff(1)
+    branch = finish4(kc)
+    copy(kc, p4_sum, p4_chip, chip_of(1 - y, 2)).wait_send()
+    for i in range(2):
+        copy(k4 + i, p4.at[i, 1 - core], p4_core.at[i], partner).wait_send()
+
+    bran[...] = branch
+    hidden = act[shard].astype(F32) + branch * rms_factor(branch) * gain(1)
+    hid[...] = hidden
+    low = (hidden * rms_factor(hidden) * gain(2)).astype(BF16)
+
+    me = m * 2 + y
+
+    def gather8(full, value):
+        kg = slots(8)
+        full[me, core] = value
+        send(kg + 4, full.at[me, core], full.at[me, core], partner)
+        for i in range(1, 4):
+            send(kg + i, full.at[me, core], full.at[me, core], chip_of((me + i) % 4, 4))
+        return kg
+
+    def pass8(kg, full, i):
+        k = (me - i + 4) % 4
+        arrive(kg + i, full.at[k, core])
+        copy(kg + 4 + i, full.at[k, core], full.at[k, core], partner).start()
+
+    def meet8(kg, full, i):
+        k = (me - i + 4) % 4
+        arrive(kg + 4 + i, full.at[k, 1 - core])
+
+    def settle8(kg, full):
+        for i in range(1, 4):
+            k = (me - i + 4) % 4
+            copy(kg + 4 + i, full.at[k, core], full.at[k, core], partner).wait_send()
+
+    def give8(ko, i):
+        k = (me - i + 4) % 4
+        copy(ko + i, p8.at[k, 1 - core], p8_core.at[i], partner).start()
+
+    def push8(ko, i):
+        k = (me - i + 4) % 4
+        arrive(ko + i, p8_core.at[i])
+        p8_sum[i - 1] = (
+            p8[k, core].astype(F32) + p8_core[i].astype(F32)
+        ).astype(BF16)
+        copy(ko + 4 + i, p8_sum.at[i - 1], p8_chip.at[i - 1], chip_of(k, 4)).start()
+
+    def finish8(ko):
+        arrive(ko, p8_core.at[0])
+        total = p8[me, core].astype(F32) + p8_core[0].astype(F32)
+        for i in range(1, 4):
+            arrive(ko + 4 + i, p8_chip.at[i - 1])
+            total = total + p8_chip[i - 1].astype(F32)
+        for i in range(4):
+            copy(ko + i, p8.at[0, 1 - core], p8_core.at[i], partner).wait_send()
+        for i in range(1, 4):
+            copy(ko + 4 + i, p8_sum.at[0], p8_chip.at[0], partner).wait_send()
+        return total
+
+    kx = gather8(xg, low)
+    for step in range(2, C):
+        relay_ff(step)
+    own_ff.wait()
+    own_cot.wait()
+    arrive(kf, wf.at[:, rows_of(1 - f, c)])
+    for step in range(1, C):
+        arrive(kf + C + step, wf.at[:, rows_of(1 - f, (c - step + C) % C)])
+
+    root = 0.7978845608028654
+    ko = slots(8)
+
+    def forward(i, _):
+        k = (me - i + 4) % 4
+        meet8(kx, xg, i)
+        x = xg[k].reshape(2 * S, D)
+        gate = mm(x, wf[0])
+        up = mm(x, wf[1])
+
+        @pl.when(i < 3)
+        def _():
+            pass8(kx, xg, i + 1)
+
+        square = gate * gate
+        bent = jnp.tanh(root * gate * (1.0 + 0.044715 * square))
+        ramp = 0.5 * (1.0 + bent)
+        gelu = gate * ramp
+        slope = ramp + 0.5 * gate * (1.0 - bent * bent) * root * (1.0 + 3 * 0.044715 * square)
+        gel[k] = gelu.astype(BF16)
+        upg[k] = (up * slope).astype(BF16)
+        low = (gelu * up).astype(BF16)
+        active[k] = low
+        p8[k] = contract_last(low, wf[2]).astype(BF16).reshape(2, S, D)
+        give8(ko, i)
+
+        @pl.when(i > 1)
+        def _():
+            push8(ko, i - 1)
+
+        return 0
+
+    lax.fori_loop(0, 4, forward, 0)
+    push8(ko, 3)
+    settle8(kx, xg)
+    down = finish8(ko)
+
+    factor = rms_factor(down)
+    grad = cot[...].astype(F32)
+    result = (hid[...] + down * factor * gain(3)).astype(BF16)
+    d_down, gain_3 = rms_backward(grad, down, factor, gain(3))
+    gain_mine[3:4] = gain_3
+    kd = gather8(dd, d_down.astype(BF16))
+
+    def share4(full, value):
+        kb = slots(4)
+        full[y, core] = value
+        for i in range(1, 4):
+            send(kb + i, full.at[y, core], full.at[y, core], {"tensor": (t + i) % 4})
+        return kb
+
+    def meet4(kb, full):
+        for i in range(1, 4):
+            k = (t - i + 4) % 4
+            arrive(kb + i, full.at[k // 2, k % 2])
+
+    kr = share4(block_all, result)
+    ko2 = slots(8)
+
+    def backward(i, _):
+        k = (me - i + 4) % 4
+        meet8(kd, dd, i)
+        low = dd[k].reshape(2 * S, D)
+        d_active = mm(low, wf[2])
+
+        @pl.when(i < 3)
+        def _():
+            pass8(kd, dd, i + 1)
+
+        d_gate = (d_active * upg[k].astype(F32)).astype(BF16)
+        d_up = (d_active * gel[k].astype(F32)).astype(BF16)
+        upg[k] = d_gate
+        gel[k] = d_up
+        p8[k] = (
+            (contract_last(d_gate, wf[0]) + contract_last(d_up, wf[1]))
+            .astype(BF16)
+            .reshape(2, S, D)
+        )
+        give8(ko2, i)
+
+        @pl.when(i > 1)
+        def _():
+            push8(ko2, i - 1)
+
+        return 0
+
+    lax.fori_loop(0, 4, backward, 0)
+    push8(ko2, 3)
+    settle8(kd, dd)
+
+    settle()
+    gall = wf
+    kw = slots(3)
+    kz = slots(3 * C)
+    mine_x = pl.ds(pl.multiple_of(f * C * R, C * R), C * R)
+    theirs_x = pl.ds(pl.multiple_of((1 - f) * C * R, C * R), C * R)
+
+    def weight_grad(w, left, right):
+        def tile(n, _):
+            cols = pl.ds(pl.multiple_of(n * LANES, LANES), LANES)
+            block = left[:, :, :, cols].reshape(8 * S, LANES)
+            gall[w, pl.ds(pl.multiple_of(n * LANES, LANES), LANES)] = contract_first(
+                block, right[...].reshape(8 * S, U)
+            ).astype(BF16)
+            return 0
+
+        lax.fori_loop(0, D // LANES, tile, 0)
+        send(kw + w, gall.at[w, theirs_x], gall_x.at[w], across)
+
+    def weight_push(w):
+        arrive(kw + w, gall_x.at[w])
+
+        def add(n, _):
+            rows = pl.ds(pl.multiple_of(f * C * R + n * R, R), R)
+            part = pl.ds(pl.multiple_of(n * R, R), R)
+            gall[w, rows] = (
+                gall[w, rows].astype(F32) + gall_x[w, part].astype(F32)
+            ).astype(BF16)
+            return 0
+
+        lax.fori_loop(0, C, add, 0)
+        for step in range(1, C):
+            send(
+                kz + w * C + step,
+                gall.at[w, rows_of(f, (c + step) % C)],
+                gall_z.at[step - 1, w],
+                along(step),
+            )
+
+    def weight_end(w):
+        same = gall[w, rows_of(f, c)].astype(F32)
+        other = jnp.zeros((R, U), F32)
+        for step in range(1, C):
+            arrive(kz + w * C + step, gall_z.at[step - 1, w])
+            if step % 2:
+                other = other + gall_z[step - 1, w].astype(F32)
+            else:
+                same = same + gall_z[step - 1, w].astype(F32)
+        ff_stage[m] = same
+        ff_stage[1 - m] = other
+        saved = pltpu.make_async_copy(ff_stage, out_ff.at[w], ls.at[5])
+        saved.start()
+        saved.wait()
+
+    weight_grad(2, dd, active)
+    d_normed = finish8(ko2)
+    hidden = hid[...]
+    d_hidden, gain_2 = rms_backward(d_normed, hidden, rms_factor(hidden), gain(2))
+    d_hidden = cot[...].astype(F32) + d_hidden
+    dhid[...] = d_hidden
+    gain_mine[2:3] = gain_2
+    branch = bran[...]
+    d_branch, gain_1 = rms_backward(d_hidden, branch, rms_factor(branch), gain(1))
+    gain_mine[1:2] = gain_1
+    kb = share4(db, d_branch.astype(BF16))
+    weight_grad(0, xg, upg)
+    meet4(kb, db)
+
+    def scores_back(i, gain_q):
+        rows = pl.ds(pl.multiple_of(i * half, half), half)
+        d_mixed = mm(db[i].reshape(half, D), wa[:, 3 * HD : 4 * HD]).astype(BF16)
+        dmix[rows] = d_mixed
+        p = probs[rows]
+        d_probs = contract_last(d_mixed, kv[:, HD:])
+        inner = jnp.sum(p * d_probs, axis=1, keepdims=True)
+        low = (p * (d_probs - inner)).astype(BF16)
+        dscore[rows] = low
+        d_q = mm(low, kv[:, 0:HD]) * scale
+        raw = qraw[rows]
+        factor = rms_factor(raw)
+        d_raw, part = rms_backward(
+            turn_back(d_q, cosine[rows], sine[rows]), raw, factor, head_gain(0)
+        )
+        dq[rows] = d_raw.astype(BF16)
+        return gain_q + part
+
+    gain_q = lax.fori_loop(0, 2, scores_back, jnp.zeros((1, HD), F32))
+    kp = slots(3)
+
+    def keys_back(n, _):
+        cols = pl.ds(pl.multiple_of(n * half, half), half)
+        d_k = contract_first(dscore[:, cols], qs[...]) * scale
+        d_v = contract_first(probs[:, cols].astype(BF16), dmix[...])
+        both = jnp.concatenate([d_k, d_v], axis=1).astype(BF16)
+        kvp[n % 2, 0, n // 2] = both[0:S]
+        kvp[n % 2, 1, n // 2] = both[S:]
+        return 0
+
+    lax.fori_loop(0, 4, keys_back, 0)
+    for i in range(2):
+        send(kp + i, kvp.at[i, 1 - core], kvp_core.at[i], partner)
+
+    k4 = slots(2)
+
+    def query_back(i, _):
+        rows = pl.ds(pl.multiple_of(i * half, half), half)
+        part = contract_last(dq[rows], wa[:, 0:HD]).astype(BF16)
+        p4[i, 0] = part[0:S]
+        p4[i, 1] = part[S:]
+        copy(k4 + i, p4.at[i, 1 - core], p4_core.at[i], partner).start()
+        return 0
+
+    lax.fori_loop(0, 2, query_back, 0)
+
+    arrive(kp + (1 - y), kvp_core.at[1 - y])
+    kvp_sum[...] = (kvp[1 - y, core].astype(F32) + kvp_core[1 - y].astype(F32)).astype(BF16)
+    send(kp + 2, kvp_sum, kvp_chip, chip_of(1 - y, 2))
+    kc = sum4(k4)
+    arrive(kp + y, kvp_core.at[y])
+    arrive(kp + 2, kvp_chip)
+    d_left = (
+        kvp[y, core, 0].astype(F32) + kvp_core[y, 0].astype(F32) + kvp_chip[0].astype(F32)
+    )
+    kt = slots(1)
+    ret_out[...] = d_left.astype(BF16)
+
+    @pl.when(c > 0)
+    def _():
+        copy(kt, ret_out, ret_in, {"context": c - 1}).start()
+
+    weight_grad(1, xg, gel)
+    weight_push(2)
+
+    @pl.when(c < C - 1)
+    def _():
+        arrive(kt, ret_in)
+
+    @pl.when(c == C - 1)
+    def _():
+        ret_in[...] = jnp.zeros((S, 2 * HD), BF16)
+
+    d_kv = (
+        kvp[y, core, 1].astype(F32)
+        + kvp_core[y, 1].astype(F32)
+        + kvp_chip[1].astype(F32)
+        + ret_in[...].astype(F32)
+    )
+    raw = kraw[shard]
+    d_raw, gain_k = rms_backward(
+        turn_back(d_kv[:, :HD], cosine[shard], sine[shard]), raw, rms_factor(raw), head_gain(1)
+    )
+    d_kv = jnp.concatenate([d_raw, d_kv[:, HD:]], axis=1).astype(BF16)
+    kq = share4(dkv, d_kv)
+    d_normed = finish4(kc) + contract_last(d_kv, wa[:, HD : 3 * HD])
+    copy(kc, p4_sum, p4_chip, chip_of(1 - y, 2)).wait_send()
+    for i in range(2):
+        copy(k4 + i, p4.at[i, 1 - core], p4_core.at[i], partner).wait_send()
+    values = act[shard].astype(F32)
+    d_input, gain_0 = rms_backward(d_normed, values, rms_factor(values), gain(0))
+    ki = share4(input_all, (dhid[...] + d_input).astype(BF16))
+    gain_mine[0:1] = gain_0
+    gain_mine[4:8] = jnp.zeros((4, D), F32)
+    gain_mine[4:5, 0:HD] = gain_q
+    gain_mine[5:6, 0:HD] = gain_k
+    kn = slots(4 + 1 + C)
+    for i in range(1, 4):
+        send(kn + i, gain_mine, gain_tensor.at[i], {"tensor": (t + i) % 4})
+
+    meet4(kq, dkv)
+    kv_cols = pl.ds(pl.multiple_of(t * LANES, LANES), LANES)
+
+    def attn_grad(n, _):
+        cols = pl.ds(pl.multiple_of(n * LANES, LANES), LANES)
+        rows = pl.ds(pl.multiple_of(n * LANES, LANES), LANES)
+        left = nrm[:, cols]
+        ga[rows, 0:HD] = contract_first(
+            db[:, :, :, cols].reshape(T, LANES), mix[...]
+        ).astype(BF16)
+        ga[rows, HD : 2 * HD] = contract_first(left, dq[...]).astype(BF16)
+        ga[rows, 2 * HD :] = contract_first(
+            left, dkv[:, :, :, kv_cols].reshape(T, LANES)
+        ).astype(BF16)
+        return 0
+
+    lax.fori_loop(0, D // LANES, attn_grad, 0)
+    ke = slots(1 + C)
+    send(ke, ga.at[theirs_x], ga_x, across)
+    weight_push(0)
+    weight_push(1)
+    total = gain_mine[...]
+    for i in range(1, 4):
+        arrive(kn + i, gain_tensor.at[i])
+    for i in range(1, 4):
+        total = total + gain_tensor[i]
+    gain_tensor[0] = total
+    send(kn, gain_tensor.at[0], gain_x.at[0], across)
+    arrive(ke, ga_x)
+    ga[mine_x] = (ga[mine_x].astype(F32) + ga_x[...].astype(F32)).astype(BF16)
+    for step in range(1, C):
+        send(ke + step, ga.at[rows_of(f, (c + step) % C)], ga_z.at[step - 1], along(step))
+    arrive(kn, gain_x.at[0])
+    gain_x[1] = total + gain_x[0]
+    for step in range(1, C):
+        send(kn + 4 + step, gain_x.at[1], gain_z.at[step], along(step))
+    attn = ga[rows_of(f, c)].astype(F32)
+    for step in range(1, C):
+        arrive(ke + step, ga_z.at[step - 1])
+        attn = attn + ga_z[step - 1].astype(F32)
+    out_attn[...] = attn[:, 0 : 2 * HD]
+    kvg[t] = attn[:, 2 * HD :]
+    kh = slots(4)
+    for i in range(1, 4):
+        send(kh + i, kvg.at[t], kvg.at[t], {"tensor": (t + i) % 4})
+    total = gain_x[1]
+    for step in range(1, C):
+        arrive(kn + 4 + step, gain_z.at[step])
+        total = total + gain_z[step]
+    out_gains[...] = total
+    meet4(kr, block_all)
+    save_block = pltpu.make_async_copy(block_all, out_block, ls.at[3])
+    save_block.start()
+    meet4(ki, input_all)
+    save_input = pltpu.make_async_copy(input_all, out_input, ls.at[4])
+    save_input.start()
+    for w in (2, 0, 1):
+        weight_end(w)
+    for i in range(1, 4):
+        arrive(kh + i, kvg.at[(t - i + 4) % 4])
+    out_kv[...] = kvg[...]
+    save_block.wait()
+    save_input.wait()
+    settle()
+
+    @pl.when(c < C - 1)
+    def _():
+        copy(ks, seg_row, seg_left, {"context": c + 1}).wait_send()
+        copy(kk, kv.at[own_half], kv.at[my_half], {"context": c + 1}).wait_send()
+
+    @pl.when(c > 0)
+    def _():
+        copy(kt, ret_out, ret_in, {"context": c - 1}).wait_send()
+
+
+def fused(
+    mesh,
+    activations,
+    positions,
+    seg_ids,
+    norm_gains,
+    head_gains,
+    w_query,
+    w_keyval,
+    w_out,
+    w_gateup,
+    w_down,
+    cotangent,
+):
+    C = mesh.shape["context"]
+    T, D = activations.shape[1:]
+    R, units = w_down.shape
+    U = -(-units // (2 * LANES)) * LANES
+    S = T // 4
+    narrow = head_gains.shape[1]
+    gains = jnp.concatenate(
+        [
+            norm_gains.T,
+            jnp.pad(head_gains.T, ((0, R - narrow), (0, 0))),
+            jnp.zeros((R, LANES - 6), BF16),
+        ],
+        axis=1,
+    )
+    w_attn = jnp.concatenate([w_query, w_keyval, w_out, gains], axis=1)
+    both = jnp.concatenate([w_gateup, w_down[:, None]], axis=1)
+    both = jnp.pad(both, ((0, 0), (0, 0), (0, 2 * U - units)))
+    w_ff = both.reshape(R, 3, 2, U).transpose(2, 1, 0, 3)
+    freqs = jnp.power(10000.0, -jnp.arange(HD // 2, dtype=F32) * 2.0 / HD)
+    angles = positions[0].astype(F32)[:, None] * freqs[None, :]
+    seg_row = jnp.broadcast_to(seg_ids, (8, T))
+    seg_col = seg_ids[0][:, None]
+    operands = (
+        activations[0],
+        jnp.cos(angles),
+        jnp.sin(angles),
+        seg_row,
+        seg_col,
+        cotangent[0],
+        w_attn,
+        w_ff,
+    )
+    scratch = [
+        pltpu.VMEM((S, D), BF16),
+        pltpu.VMEM((D, D), BF16),
+        pltpu.VMEM((3, D, U), BF16),
+        pltpu.VMEM((8, T), jnp.int32),
+        pltpu.VMEM((8, D), F32),
+        pltpu.VMEM((8, HD), F32),
+        pltpu.VMEM((T, D), BF16),
+        pltpu.VMEM((T, HD), F32),
+        pltpu.VMEM((T, HD), F32),
+        pltpu.VMEM((T, HD), BF16),
+        pltpu.VMEM((2 * T, 2 * HD), BF16),
+        pltpu.VMEM((T, 2 * T), F32),
+        pltpu.VMEM((T, HD), BF16),
+        pltpu.VMEM((2, 2, S, D), BF16),
+        pltpu.VMEM((2, S, D), BF16),
+        pltpu.VMEM((S, D), BF16),
+        pltpu.VMEM((S, D), BF16),
+        pltpu.VMEM((S, D), F32),
+        pltpu.VMEM((S, D), F32),
+        pltpu.VMEM((4, 2, S, D), BF16),
+        pltpu.VMEM((4, 2 * S, U), BF16),
+        pltpu.VMEM((4, 2 * S, U), BF16),
+        pltpu.VMEM((4, 2 * S, U), BF16),
+        pltpu.VMEM((4, 2, S, D), BF16),
+        pltpu.VMEM((4, S, D), BF16),
+        pltpu.VMEM((3, S, D), BF16),
+        pltpu.VMEM((3, S, D), BF16),
+        pltpu.VMEM((4, 2, S, D), BF16),
+        pltpu.VMEM((S, D), F32),
+        pltpu.VMEM((2, 2, S, D), BF16),
+        pltpu.VMEM((T, 2 * T), BF16),
+        pltpu.VMEM((T, HD), BF16),
+        pltpu.VMEM((T, HD), BF16),
+        pltpu.VMEM((2, 2, 2, S, 2 * HD), BF16),
+        pltpu.VMEM((2, 2, S, 2 * HD), BF16),
+        pltpu.VMEM((2, S, 2 * HD), BF16),
+        pltpu.VMEM((2, S, 2 * HD), BF16),
+        pltpu.VMEM((S, 2 * HD), BF16),
+        pltpu.VMEM((S, 2 * HD), BF16),
+        pltpu.VMEM((2, 2, S, 2 * HD), BF16),
+        pltpu.VMEM((3, C * R, U), BF16),
+        pltpu.VMEM((C - 1, 3, R, U), BF16),
+        pltpu.VMEM((D, 2 * HD + LANES), BF16),
+        pltpu.VMEM((C * R, 2 * HD + LANES), BF16),
+        pltpu.VMEM((C - 1, R, 2 * HD + LANES), BF16),
+        pltpu.VMEM((4, R, LANES), F32),
+        pltpu.VMEM((2, R, U), F32),
+        pltpu.VMEM((8, D), F32),
+        pltpu.VMEM((4, 8, D), F32),
+        pltpu.VMEM((2, 8, D), F32),
+        pltpu.VMEM((C, 8, D), F32),
+        pltpu.VMEM((2, 2, S, D), BF16),
+        pltpu.VMEM((2, 2, S, D), BF16),
+        pltpu.SemaphoreType.DMA((SEMAPHORES,)),
+        pltpu.SemaphoreType.DMA((SEMAPHORES,)),
+        pltpu.SemaphoreType.DMA((6,)),
+    ]
+    vmem = pl.BlockSpec(memory_space=pltpu.VMEM)
+    anywhere = pl.BlockSpec(memory_space=pl.ANY)
+    results = (
+        jax.ShapeDtypeStruct((2, 2, S, D), BF16),
+        jax.ShapeDtypeStruct((2, 2, S, D), BF16),
+        jax.ShapeDtypeStruct((8, D), F32),
+        jax.ShapeDtypeStruct((3, 2, R, U), F32),
+        jax.ShapeDtypeStruct((R, 2 * HD), F32),
+        jax.ShapeDtypeStruct((4, R, LANES), F32),
+    )
+    sizes = {"context": C, "tokens": T, "width": D, "rows": R, "units": U}
+    block_out, input_grad, gain_sums, ff_grads, attn_grads, kv_grads = pl.pallas_call(
+        functools.partial(fused_kernel, sizes),
+        out_shape=results,
+        in_specs=[vmem] * 5 + [anywhere] * 3,
+        out_specs=[anywhere] * 2 + [vmem, anywhere, vmem, vmem],
+        scratch_shapes=scratch,
+        compiler_params=pltpu.CompilerParams(
+            collective_id=0, has_side_effects=True, vmem_limit_bytes=67043328
+        ),
+    )(*operands)
+    owner = lax.axis_index(("fsdp", "context"))
+    norm_grad = lax.dynamic_slice(gain_sums, (0, owner * R), (4, R))
+    head_grad = lax.dynamic_slice(gain_sums, (4, owner * narrow), (2, narrow))
+    ff = ff_grads.transpose(2, 0, 1, 3).reshape(R, 3, 2 * U)[:, :, :units]
+    return (
+        block_out.reshape(1, T, D),
+        input_grad.reshape(1, T, D),
+        norm_grad,
+        head_grad,
+        attn_grads[:, HD:],
+        kv_grads.transpose(1, 0, 2).reshape(R, 2 * HD),
+        attn_grads[:, :HD],
+        ff[:, :2],
+        ff[:, 2],
+    )
+
+
+def block(mesh, *arrays):
+    tokens, rows = arrays[0].shape[1], arrays[9].shape[0]
+    fits = (
+        mesh.shape["fsdp"] == 2
+        and mesh.shape["tensor"] == 4
+        and mesh.shape["context"] == 4
+        and tokens == WINDOW
+        and rows % 16 == 0
+        and arrays[5].shape[1] == HD
+        and arrays[6].shape[1] == 4 * LANES
+    )
+    return fused(mesh, *arrays) if fits else shards(*arrays)
 
 
 def shards(
@@ -286,7 +1168,7 @@
 
 def solution(mesh):
     return jax.shard_map(
-        shards,
+        functools.partial(block, mesh),
         mesh=mesh,
         in_specs=(
             P("fsdp", "context", None),

time: 1120 us -> 376 us (0.34)
  waiting for transfers between devices: 796 us -> 0 us
  Pallas kernels: 0 us -> 343 us
  blocking collectives: 120 us -> 0 us
  matrix products: 72.4 us -> 0 us
  other arithmetic: 49.1 us -> 4.86 us
  local copies, waits for them, and re-layouts: 50.5 us -> 27.2 us
  between operations: 15.3 us -> 0.74 us
    pallas_call x0 -> x1, Pallas kernels: none -> 343 us  [fused(): pl.pallas_call(functools.partial(fused_kernel, sizes), out_shape=results,...]
    unnamed x18 -> x0, waiting for transfers between devices: 256 us -> none
    reduce_scatter x3 -> x0, waiting for transfers between devices: 215 us -> none  [the longest x1 83.7 us: shards(): lax.psum_scatter(part.astype(jnp.bfloat16), ('fsdp', 'context'), scatter_...]
    all_gather x3 -> x0, waiting for transfers between devices: 178 us -> none  [the longest x1 119 us: shards(): lax.all_gather(w_gateup, ('fsdp', 'context'), axis=0, tiled=True)]
    psum x4 -> x0, waiting for transfers between devices: 135 us -> none  [the longest x1 36.4 us: shards(): lax.psum(d_normed_part.astype(jnp.bfloat16), 'tensor').astype(jnp.float32)]
    all_gather x4 -> x0, blocking collectives: 112 us -> none  [the longest x1 33.8 us: shards(): lax.all_gather(w_out, ('fsdp', 'context'), axis=0, tiled=True)]
    dot_general x21 -> x0, matrix products: 72.4 us -> none  [the longest x4 14.2 us: contract_first(): lax.dot_general(left_side, right_side, (((0,), (0,)), ((), ())), preferre...]
    unnamed x180 -> x13, local copies, waits for them, and re-layouts: 39.6 us -> 7.17 us
  transfers between devices with their start and end apart: 17 -> 0, of which waited for: 14 -> 0; matrix products, arithmetic and copies ran while one was open for 9% -> 0% of each run, Pallas kernels for 0% -> 0%
where the time goes in v2:
time: 376 us
  Pallas kernels  343 us (91%)
  local copies, waits for them, and re-layouts  27.2 us (7%)
  other arithmetic  4.86 us (1%)
    pallas_call x1, Pallas kernels, fused(): pl.pallas_call(functools.partial(fused_kernel, sizes), out_shape=results,...  343 us

profile of v2, /device:TPU:0, one launch (start us, length us, event | category | flops | bytes accessed | tf_op | source)
XLA Modules:
  0.0 376.0 jit_solution(2787089719148781191)
XLA Ops:
  0.6 0.0 copy-start.3
  0.7 0.0 copy-start.2
  0.7 0.8 convert_element_type.14
  1.5 0.7 copy.25
  2.2 1.3 broadcast_in_dim.16.seg_row
  3.5 0.8 copy.24
  4.4 1.8 concatenate.6.w_attn
  6.2 1.5 copy.29.seg_col
  7.7 1.8 multiply_sine_fusion
  9.5 0.0 copy-done.3
  9.5 0.8 copy.26
  10.3 0.0 copy-done.2
  10.3 2.3 fusion.2
  12.6 2.5 reshape.50
  15.1 2.7 copy.39
  17.8 343.2 %shard_map.178 = (bf16[2,2,128,1152]{3,2,1,0:T(8,128)(2,1)}, bf16[2,2,128,1152]{3,2,1,0:T(8,128)(2,1)}, f32[8,1152]{1,0:T(8,128)}, f32[3,2,144,896]{3,2,1,0:T(8,...) custom-call(bf16[512,1152]{1,0:T(8,128)(2,1)} %bitcast.30, f32[512,128]{1,0:T(8,128)} %get-tuple-element.42.cosine, ...), custom_call_target="tpu_custom_call" | custom-call | tf_op jit(solution)/shard_map/pallas_call | solution.py:896
  361.0 1.3 constant_dynamic-slice_fusion
  362.3 1.4 constant_dynamic-slice_fusion.1
  363.7 1.7 copy_bitcast_fusion.1
  365.4 1.7 fusion.3
  367.1 2.1 copy.36
  369.2 1.0 slice_bitcast_fusion
  370.2 0.1 slice.19
  370.3 0.0 copy-start.1
  370.3 2.9 copy.32
  373.2 0.0 copy-done.1
  373.2 0.0 copy-start
  373.2 1.0 copy.42
  374.3 0.7 copy-done
  374.9 1.0 copy.43
  (3 shorter events, 0.0 us)
Async XLA Ops:
  0.6 8.9 %copy-start.3 = (bf16[144,1728]{1,0:T(8,128)(2,1)S(1)}, bf16[144,1728]{1,0:T(8,128)(2,1)}, u32[]{:S(2)}) copy-start(bf16[144,1728]{1,0:T(8,128)(2,1)} %param.20) | copy-start | bytes 1492996
  0.7 9.7 %copy-start.2 = (bf16[144,2,1728]{2,1,0:T(2,128)(2,1)S(1)}, bf16[144,2,1728]{2,1,0:T(2,128)(2,1)}, u32[]{:S(2)}) copy-start(bf16[144,2,1728]{2,1,0:T(2,128)(2,1)} %param.19) | copy-start | bytes 2985988
  370.3 2.9 copy-start.1
  373.2 1.7 copy-start

commit v3 on v2

--- a/solution.py
+++ b/solution.py
@@ -60,7 +60,7 @@
 F32 = jnp.float32
 BF16 = jnp.bfloat16
 LANES = 128
-SEMAPHORES = 112
+SEMAPHORES = 160
 
 
 def mm(left, right):
@@ -98,7 +98,10 @@
     seg_row,
     seg_col,
     cot_all,
-    w_attn,
+    w_query,
+    w_keyval,
+    w_out,
+    gain_cols,
     w_ff,
     out_block,
     out_input,
@@ -114,7 +117,7 @@
     head_rows,
     nrm,
     qraw,
-    kraw,
+    kv_raw,
     qs,
     kv,
     probs,
@@ -145,7 +148,8 @@
     kvp_chip,
     ret_out,
     ret_in,
-    dkv,
+    dkv_mine,
+    dkv_cols,
     gall_x,
     gall_z,
     ga,
@@ -226,31 +230,74 @@
     pl.semaphore_wait(barrier, len(greeted))
 
     mine = rows_of(f, c)
-    own_attn = pltpu.make_async_copy(w_attn, wa.at[mine], ls.at[0])
-    own_attn.start()
-    ka = slots(2 * C)
+    kv_cols = pl.ds(pl.multiple_of(t * LANES, LANES), LANES)
+    attn_parts = (
+        (w_query, slice(0, HD)),
+        (w_keyval.at[:, kv_cols], slice(HD, HD + LANES)),
+        (w_out, slice(HD + LANES, 2 * HD + LANES)),
+        (gain_cols, slice(2 * HD + LANES, 2 * HD + 2 * LANES)),
+    )
+    q_cols, kv_part, o_cols = (cols for _, cols in attn_parts[:3])
+    local = []
+    for n, (part, cols) in enumerate(attn_parts):
+        local.append(pltpu.make_async_copy(part, wa.at[mine, cols], ls.at[6 + n]))
+        local[-1].start()
+    ka = slots(4 * C)
+    kar = slots(C)
     for step in range(1, C):
-        send(ka + step, w_attn, wa.at[mine], along(step))
-    send(ka, w_attn, wa.at[mine], across)
+        for n, (part, cols) in enumerate(attn_parts):
+            send(ka + 4 * step + n, part, wa.at[mine, cols], along(step))
+    for n, (part, cols) in enumerate(attn_parts):
+        send(ka + n, part, wa.at[mine, cols], across)
     ks = slots(1)
 
     @pl.when(c < C - 1)
     def _():
         copy(ks, seg_row, seg_left, {"context": c + 1}).start()
 
+    kf = slots(6 * C)
+
+    def send_ff(w):
+        k = kf + 2 * C * w
+        for step in range(1, C):
+            send(k + step, w_ff.at[(c + step) % 2, w], wf.at[w, mine], along(step))
+        send(k, w_ff.at[m, w], wf.at[w, mine], across)
+
+    def relay_ff(w, step):
+        k = kf + 2 * C * w
+        part = wf.at[w, rows_of(f, (c - step + C) % C)]
+        arrive(k + step, part)
+        copy(k + C + step, part, part, across).start()
+
+    def meet_ff(w):
+        k = kf + 2 * C * w
+        arrive(k, wf.at[w, rows_of(1 - f, c)])
+        for step in range(1, C):
+            arrive(k + C + step, wf.at[w, rows_of(1 - f, (c - step + C) % C)])
+
+    def settle_ff(w):
+        k = kf + 2 * C * w
+        for step in range(1, C):
+            part = wf.at[w, rows_of(f, (c - step + C) % C)]
+            copy(k + C + step, part, part, across).wait_send()
+
+    send_ff(0)
     shard = pl.ds(pl.multiple_of(t * S, S), S)
     own_cot = pltpu.make_async_copy(cot_all.at[shard], cot, ls.at[2])
     own_cot.start()
     own_ff = pltpu.make_async_copy(w_ff.at[m], wf.at[:, mine], ls.at[1])
     own_ff.start()
-    own_attn.wait()
     for step in range(1, C):
-        block = wa.at[rows_of(f, (c - step + C) % C)]
-        arrive(ka + step, block)
-        send(ka + C + step, block, block, across)
-    arrive(ka, wa.at[rows_of(1 - f, c)])
+        other = rows_of(f, (c - step + C) % C)
+        for n, (_, cols) in enumerate(attn_parts):
+            arrive(ka + 4 * step + n, wa.at[other, cols])
+        send(kar + step, wa.at[other], wa.at[other], across)
+    for moved in local:
+        moved.wait()
+    for n, (_, cols) in enumerate(attn_parts):
+        arrive(ka + n, wa.at[rows_of(1 - f, c), cols])
     for step in range(1, C):
-        arrive(ka + C + step, wa.at[rows_of(1 - f, (c - step + C) % C)])
+        arrive(kar + step, wa.at[rows_of(1 - f, (c - step + C) % C)])
 
     @pl.when(c > 0)
     def _():
@@ -261,7 +308,7 @@
         seg_left[...] = jnp.full(seg_left.shape, -1, jnp.int32)
         kv[0:T] = jnp.zeros((T, 2 * HD), BF16)
 
-    gain_t = jnp.transpose(wa[:, 4 * HD :].astype(F32))
+    gain_t = jnp.transpose(wa[:, 2 * HD + LANES :].astype(F32))
     gain_rows[...] = gain_t[0:8]
     narrow = HD // (2 * C)
     here = lax.broadcasted_iota(jnp.int32, (D, HD), 0)
@@ -284,20 +331,39 @@
         values = act[rows].astype(F32)
         low = (values * rms_factor(values) * gain(0)).astype(BF16)
         nrm[rows] = low
-        raw_q = mm(low, wa[:, 0:HD])
-        raw_kv = mm(low, wa[:, HD : 3 * HD])
-        raw_k = raw_kv[:, :HD]
+        kv_raw[t, rows] = mm(low, wa[:, kv_part]).astype(BF16)
+        return 0
+
+    lax.fori_loop(0, 2, project, 0)
+    ku = slots(4)
+    for i in range(1, 4):
+        send(ku + i, kv_raw.at[t], kv_raw.at[t], {"tensor": (t + i) % 4})
+
+    def query(i, _):
+        rows = pl.ds(pl.multiple_of(i * half, half), half)
+        raw_q = mm(nrm[rows], wa[:, q_cols])
         qraw[rows] = raw_q
-        kraw[rows] = raw_k
-        cos, sin = cosine[rows], sine[rows]
-        qs[rows] = turn(raw_q * rms_factor(raw_q) * head_gain(0), cos, sin).astype(BF16)
+        qs[rows] = turn(
+            raw_q * rms_factor(raw_q) * head_gain(0), cosine[rows], sine[rows]
+        ).astype(BF16)
+        return 0
+
+    lax.fori_loop(0, 2, query, 0)
+    for i in range(1, 4):
+        arrive(ku + i, kv_raw.at[(t - i + 4) % 4])
+
+    def key(i, _):
+        rows = pl.ds(pl.multiple_of(i * half, half), half)
+        raw_k = jnp.concatenate([kv_raw[0, rows], kv_raw[1, rows]], axis=1).astype(F32)
         own = pl.ds(pl.multiple_of(T + i * half, half), half)
-        kv[own, 0:HD] = turn(raw_k * rms_factor(raw_k) * head_gain(1), cos, sin).astype(BF16)
-        kv[own, HD:] = raw_kv[:, HD:].astype(BF16)
+        kv[own, 0:HD] = turn(
+            raw_k * rms_factor(raw_k) * head_gain(1), cosine[rows], sine[rows]
+        ).astype(BF16)
+        kv[own, HD : HD + LANES] = kv_raw[2, rows]
+        kv[own, HD + LANES :] = kv_raw[3, rows]
         return 0
 
-    lax.fori_loop(0, 2, project, 0)
-
+    lax.fori_loop(0, 2, key, 0)
     kk = slots(2)
     my_half = pl.ds(pl.multiple_of(core * half, half), half)
     other_half = pl.ds(pl.multiple_of((1 - core) * half, half), half)
@@ -307,10 +373,9 @@
     def _():
         copy(kk, kv.at[own_half], kv.at[my_half], {"context": c + 1}).start()
 
-    kf = slots(2 * C)
+    send_ff(1)
     for step in range(1, C):
-        send(kf + step, w_ff.at[(c + step) % 2], wf.at[:, mine], along(step))
-    send(kf, w_ff.at[m], wf.at[:, mine], across)
+        relay_ff(0, step)
 
     @pl.when(c > 0)
     def _():
@@ -345,18 +410,13 @@
         mixed = mm(left.astype(BF16), kv[0:T, HD:]) + mm(own.astype(BF16), kv[T:, HD:])
         mixed = mixed.astype(BF16)
         mix[rows] = mixed
-        part = contract_last(mixed, wa[:, 3 * HD : 4 * HD]).astype(BF16)
+        part = contract_last(mixed, wa[:, o_cols]).astype(BF16)
         p4[i, 0] = part[0:S]
         p4[i, 1] = part[S:]
         copy(k4 + i, p4.at[i, 1 - core], p4_core.at[i], partner).start()
         return 0
 
     lax.fori_loop(0, 2, attend, 0)
-
-    def relay_ff(step):
-        block = wf.at[:, rows_of(f, (c - step + C) % C)]
-        arrive(kf + step, block)
-        send(kf + C + step, block, block, across)
 
     def sum4(k):
         kc = slots(1)
@@ -377,7 +437,8 @@
         )
 
     kc = sum4(k4)
-    relay_ff(1)
+    relay_ff(1, 1)
+    relay_ff(1, 2)
     branch = finish4(kc)
     copy(kc, p4_sum, p4_chip, chip_of(1 - y, 2)).wait_send()
     for i in range(2):
@@ -437,14 +498,12 @@
         return total
 
     kx = gather8(xg, low)
-    for step in range(2, C):
-        relay_ff(step)
+    send_ff(2)
+    relay_ff(1, 3)
     own_ff.wait()
     own_cot.wait()
-    arrive(kf, wf.at[:, rows_of(1 - f, c)])
-    for step in range(1, C):
-        arrive(kf + C + step, wf.at[:, rows_of(1 - f, (c - step + C) % C)])
-
+    meet_ff(0)
+    meet_ff(1)
     root = 0.7978845608028654
     ko = slots(8)
 
@@ -466,9 +525,20 @@
         slope = ramp + 0.5 * gate * (1.0 - bent * bent) * root * (1.0 + 3 * 0.044715 * square)
         gel[k] = gelu.astype(BF16)
         upg[k] = (up * slope).astype(BF16)
-        low = (gelu * up).astype(BF16)
-        active[k] = low
-        p8[k] = contract_last(low, wf[2]).astype(BF16).reshape(2, S, D)
+        active[k] = (gelu * up).astype(BF16)
+
+        @pl.when(i > 0)
+        def _():
+            relay_ff(2, i)
+
+        return 0
+
+    lax.fori_loop(0, 4, forward, 0)
+    meet_ff(2)
+
+    def lower(i, _):
+        k = (me - i + 4) % 4
+        p8[k] = contract_last(active[k], wf[2]).astype(BF16).reshape(2, S, D)
         give8(ko, i)
 
         @pl.when(i > 1)
@@ -477,7 +547,7 @@
 
         return 0
 
-    lax.fori_loop(0, 4, forward, 0)
+    lax.fori_loop(0, 4, lower, 0)
     push8(ko, 3)
     settle8(kx, xg)
     down = finish8(ko)
@@ -489,19 +559,19 @@
     gain_mine[3:4] = gain_3
     kd = gather8(dd, d_down.astype(BF16))
 
-    def share4(full, value):
-        kb = slots(4)
-        full[y, core] = value
-        for i in range(1, 4):
-            send(kb + i, full.at[y, core], full.at[y, core], {"tensor": (t + i) % 4})
+    def share4(full):
+        kb = slots(3)
+        send(kb, full.at[y, core], full.at[y, core], chip_of(1 - y, 2))
+        send(kb + 1, full.at[y, core], full.at[y, core], partner)
         return kb
 
     def meet4(kb, full):
-        for i in range(1, 4):
-            k = (t - i + 4) % 4
-            arrive(kb + i, full.at[k // 2, k % 2])
-
-    kr = share4(block_all, result)
+        arrive(kb, full.at[1 - y, core])
+        send(kb + 2, full.at[1 - y, core], full.at[1 - y, core], partner)
+        arrive(kb + 1, full.at[y, 1 - core])
+        arrive(kb + 2, full.at[1 - y, 1 - core])
+
+    block_all[y, core] = result
     ko2 = slots(8)
 
     def backward(i, _):
@@ -536,49 +606,69 @@
     settle8(kd, dd)
 
     settle()
+    for w in range(3):
+        settle_ff(w)
     gall = wf
-    kw = slots(3)
-    kz = slots(3 * C)
     mine_x = pl.ds(pl.multiple_of(f * C * R, C * R), C * R)
     theirs_x = pl.ds(pl.multiple_of((1 - f) * C * R, C * R), C * R)
-
-    def weight_grad(w, left, right):
+    chunks = (
+        (2, 0, 256),
+        (2, 256, 512),
+        (2, 512, U),
+        (0, 0, 512),
+        (0, 512, U),
+        (1, 0, 512),
+        (1, 512, U),
+    )
+    kw = slots(len(chunks))
+    kz = slots(len(chunks) * C)
+
+    def weight_grad(w, left, right, early):
         def tile(n, _):
             cols = pl.ds(pl.multiple_of(n * LANES, LANES), LANES)
             block = left[:, :, :, cols].reshape(8 * S, LANES)
-            gall[w, pl.ds(pl.multiple_of(n * LANES, LANES), LANES)] = contract_first(
-                block, right[...].reshape(8 * S, U)
-            ).astype(BF16)
+            gall[w, cols] = contract_first(block, right[...].reshape(8 * S, U)).astype(BF16)
             return 0
 
-        lax.fori_loop(0, D // LANES, tile, 0)
-        send(kw + w, gall.at[w, theirs_x], gall_x.at[w], across)
-
-    def weight_push(w):
-        arrive(kw + w, gall_x.at[w])
+        first = D // LANES // 2
+        lax.fori_loop(0, first + 1, lambda n, _: tile(n + first * (1 - f), _), 0)
+        for q in early:
+            weight_send(q)
+        lax.fori_loop(0, first, lambda n, _: tile(n + (first + 1) * f, _), 0)
+
+    def weight_send(q):
+        w, low, high = chunks[q]
+        send(kw + q, gall.at[w, theirs_x, low:high], gall_x.at[w, :, low:high], across)
+
+    def weight_push(q):
+        w, low, high = chunks[q]
+        arrive(kw + q, gall_x.at[w, :, low:high])
 
         def add(n, _):
             rows = pl.ds(pl.multiple_of(f * C * R + n * R, R), R)
             part = pl.ds(pl.multiple_of(n * R, R), R)
-            gall[w, rows] = (
-                gall[w, rows].astype(F32) + gall_x[w, part].astype(F32)
+            gall[w, rows, low:high] = (
+                gall[w, rows, low:high].astype(F32) + gall_x[w, part, low:high].astype(F32)
             ).astype(BF16)
             return 0
 
         lax.fori_loop(0, C, add, 0)
         for step in range(1, C):
             send(
-                kz + w * C + step,
-                gall.at[w, rows_of(f, (c + step) % C)],
-                gall_z.at[step - 1, w],
+                kz + q * C + step,
+                gall.at[w, rows_of(f, (c + step) % C), low:high],
+                gall_z.at[step - 1, w, :, low:high],
                 along(step),
             )
 
     def weight_end(w):
+        for q, (chunk, low, high) in enumerate(chunks):
+            for step in range(1, C):
+                if chunk == w:
+                    arrive(kz + q * C + step, gall_z.at[step - 1, w, :, low:high])
         same = gall[w, rows_of(f, c)].astype(F32)
         other = jnp.zeros((R, U), F32)
         for step in range(1, C):
-            arrive(kz + w * C + step, gall_z.at[step - 1, w])
             if step % 2:
                 other = other + gall_z[step - 1, w].astype(F32)
             else:
@@ -589,7 +679,7 @@
         saved.start()
         saved.wait()
 
-    weight_grad(2, dd, active)
+    weight_grad(2, dd, active, (0, 1, 2))
     d_normed = finish8(ko2)
     hidden = hid[...]
     d_hidden, gain_2 = rms_backward(d_normed, hidden, rms_factor(hidden), gain(2))
@@ -599,13 +689,17 @@
     branch = bran[...]
     d_branch, gain_1 = rms_backward(d_hidden, branch, rms_factor(branch), gain(1))
     gain_mine[1:2] = gain_1
-    kb = share4(db, d_branch.astype(BF16))
-    weight_grad(0, xg, upg)
+    db[y, core] = d_branch.astype(BF16)
+    kb = share4(db)
+    weight_grad(0, xg, upg, (3, 4))
+    weight_push(0)
+    weight_grad(1, xg, gel, (5,))
+    weight_push(1)
     meet4(kb, db)
 
     def scores_back(i, gain_q):
         rows = pl.ds(pl.multiple_of(i * half, half), half)
-        d_mixed = mm(db[i].reshape(half, D), wa[:, 3 * HD : 4 * HD]).astype(BF16)
+        d_mixed = mm(db[i].reshape(half, D), wa[:, o_cols]).astype(BF16)
         dmix[rows] = d_mixed
         p = probs[rows]
         d_probs = contract_last(d_mixed, kv[:, HD:])
@@ -637,22 +731,10 @@
     for i in range(2):
         send(kp + i, kvp.at[i, 1 - core], kvp_core.at[i], partner)
 
-    k4 = slots(2)
-
-    def query_back(i, _):
-        rows = pl.ds(pl.multiple_of(i * half, half), half)
-        part = contract_last(dq[rows], wa[:, 0:HD]).astype(BF16)
-        p4[i, 0] = part[0:S]
-        p4[i, 1] = part[S:]
-        copy(k4 + i, p4.at[i, 1 - core], p4_core.at[i], partner).start()
-        return 0
-
-    lax.fori_loop(0, 2, query_back, 0)
-
+    weight_push(2)
     arrive(kp + (1 - y), kvp_core.at[1 - y])
     kvp_sum[...] = (kvp[1 - y, core].astype(F32) + kvp_core[1 - y].astype(F32)).astype(BF16)
     send(kp + 2, kvp_sum, kvp_chip, chip_of(1 - y, 2))
-    kc = sum4(k4)
     arrive(kp + y, kvp_core.at[y])
     arrive(kp + 2, kvp_chip)
     d_left = (
@@ -665,8 +747,7 @@
     def _():
         copy(kt, ret_out, ret_in, {"context": c - 1}).start()
 
-    weight_grad(1, xg, gel)
-    weight_push(2)
+    weight_push(3)
 
     @pl.when(c < C - 1)
     def _():
@@ -682,19 +763,61 @@
         + kvp_chip[1].astype(F32)
         + ret_in[...].astype(F32)
     )
-    raw = kraw[shard]
+    raw = jnp.concatenate([kv_raw[0, shard], kv_raw[1, shard]], axis=1).astype(F32)
     d_raw, gain_k = rms_backward(
         turn_back(d_kv[:, :HD], cosine[shard], sine[shard]), raw, rms_factor(raw), head_gain(1)
     )
     d_kv = jnp.concatenate([d_raw, d_kv[:, HD:]], axis=1).astype(BF16)
-    kq = share4(dkv, d_kv)
-    d_normed = finish4(kc) + contract_last(d_kv, wa[:, HD : 3 * HD])
+    for i in range(4):
+        dkv_mine[i] = d_kv[:, i * LANES : (i + 1) * LANES]
+    kq = slots(4)
+    for i in range(1, 4):
+        k = (t + i) % 4
+        send(kq + i, dkv_mine.at[k], dkv_cols.at[t], {"tensor": k})
+    dkv_cols[t] = dkv_mine[t]
+    for i in range(1, 4):
+        arrive(kq + i, dkv_cols.at[(t - i + 4) % 4])
+
+    k4 = slots(2)
+
+    def query_back(i, _):
+        rows = pl.ds(pl.multiple_of(i * half, half), half)
+        pair = pl.ds(i * 2, 2)
+        part = contract_last(dq[rows], wa[:, q_cols])
+        part = part + contract_last(dkv_cols[pair].reshape(half, LANES), wa[:, kv_part])
+        part = part.astype(BF16)
+        p4[i, 0] = part[0:S]
+        p4[i, 1] = part[S:]
+        copy(k4 + i, p4.at[i, 1 - core], p4_core.at[i], partner).start()
+        return 0
+
+    lax.fori_loop(0, 2, query_back, 0)
+
+    def attn_grad(n, _):
+        cols = pl.ds(pl.multiple_of(n * LANES, LANES), LANES)
+        left = nrm[:, cols]
+        ga[cols, 0:HD] = contract_first(
+            db[:, :, :, cols].reshape(T, LANES), mix[...]
+        ).astype(BF16)
+        ga[cols, HD : 2 * HD] = contract_first(left, dq[...]).astype(BF16)
+        ga[cols, 2 * HD :] = contract_first(left, dkv_cols[...].reshape(T, LANES)).astype(BF16)
+        return 0
+
+    lax.fori_loop(0, D // LANES, attn_grad, 0)
+    ke = slots(1 + C)
+    send(ke, ga.at[theirs_x], ga_x, across)
+    weight_send(6)
+    kc = sum4(k4)
+    weight_push(4)
+    d_normed = finish4(kc)
     copy(kc, p4_sum, p4_chip, chip_of(1 - y, 2)).wait_send()
     for i in range(2):
         copy(k4 + i, p4.at[i, 1 - core], p4_core.at[i], partner).wait_send()
     values = act[shard].astype(F32)
     d_input, gain_0 = rms_backward(d_normed, values, rms_factor(values), gain(0))
-    ki = share4(input_all, (dhid[...] + d_input).astype(BF16))
+    input_all[y, core] = (dhid[...] + d_input).astype(BF16)
+    ki = share4(input_all)
+    kr = share4(block_all)
     gain_mine[0:1] = gain_0
     gain_mine[4:8] = jnp.zeros((4, D), F32)
     gain_mine[4:5, 0:HD] = gain_q
@@ -702,43 +825,30 @@
     kn = slots(4 + 1 + C)
     for i in range(1, 4):
         send(kn + i, gain_mine, gain_tensor.at[i], {"tensor": (t + i) % 4})
-
-    meet4(kq, dkv)
-    kv_cols = pl.ds(pl.multiple_of(t * LANES, LANES), LANES)
-
-    def attn_grad(n, _):
-        cols = pl.ds(pl.multiple_of(n * LANES, LANES), LANES)
-        rows = pl.ds(pl.multiple_of(n * LANES, LANES), LANES)
-        left = nrm[:, cols]
-        ga[rows, 0:HD] = contract_first(
-            db[:, :, :, cols].reshape(T, LANES), mix[...]
-        ).astype(BF16)
-        ga[rows, HD : 2 * HD] = contract_first(left, dq[...]).astype(BF16)
-        ga[rows, 2 * HD :] = contract_first(
-            left, dkv[:, :, :, kv_cols].reshape(T, LANES)
-        ).astype(BF16)
-        return 0
-
-    lax.fori_loop(0, D // LANES, attn_grad, 0)
-    ke = slots(1 + C)
-    send(ke, ga.at[theirs_x], ga_x, across)
-    weight_push(0)
-    weight_push(1)
+    weight_push(5)
     total = gain_mine[...]
     for i in range(1, 4):
         arrive(kn + i, gain_tensor.at[i])
-    for i in range(1, 4):
         total = total + gain_tensor[i]
     gain_tensor[0] = total
     send(kn, gain_tensor.at[0], gain_x.at[0], across)
+    meet4(ki, input_all)
+    save_input = pltpu.make_async_copy(input_all, out_input, ls.at[4])
+    save_input.start()
+    meet4(kr, block_all)
+    save_block = pltpu.make_async_copy(block_all, out_block, ls.at[3])
+    save_block.start()
     arrive(ke, ga_x)
     ga[mine_x] = (ga[mine_x].astype(F32) + ga_x[...].astype(F32)).astype(BF16)
     for step in range(1, C):
         send(ke + step, ga.at[rows_of(f, (c + step) % C)], ga_z.at[step - 1], along(step))
+    weight_push(6)
     arrive(kn, gain_x.at[0])
     gain_x[1] = total + gain_x[0]
     for step in range(1, C):
         send(kn + 4 + step, gain_x.at[1], gain_z.at[step], along(step))
+    weight_end(2)
+    weight_end(0)
     attn = ga[rows_of(f, c)].astype(F32)
     for step in range(1, C):
         arrive(ke + step, ga_z.at[step - 1])
@@ -748,19 +858,12 @@
     kh = slots(4)
     for i in range(1, 4):
         send(kh + i, kvg.at[t], kvg.at[t], {"tensor": (t + i) % 4})
+    weight_end(1)
     total = gain_x[1]
     for step in range(1, C):
         arrive(kn + 4 + step, gain_z.at[step])
         total = total + gain_z[step]
     out_gains[...] = total
-    meet4(kr, block_all)
-    save_block = pltpu.make_async_copy(block_all, out_block, ls.at[3])
-    save_block.start()
-    meet4(ki, input_all)
-    save_input = pltpu.make_async_copy(input_all, out_input, ls.at[4])
-    save_input.start()
-    for w in (2, 0, 1):
-        weight_end(w)
     for i in range(1, 4):
         arrive(kh + i, kvg.at[(t - i + 4) % 4])
     out_kv[...] = kvg[...]
@@ -806,7 +909,6 @@
         ],
         axis=1,
     )
-    w_attn = jnp.concatenate([w_query, w_keyval, w_out, gains], axis=1)
     both = jnp.concatenate([w_gateup, w_down[:, None]], axis=1)
     both = jnp.pad(both, ((0, 0), (0, 0), (0, 2 * U - units)))
     w_ff = both.reshape(R, 3, 2, U).transpose(2, 1, 0, 3)
@@ -821,19 +923,22 @@
         seg_row,
         seg_col,
         cotangent[0],
-        w_attn,
+        w_query,
+        w_keyval,
+        w_out,
+        gains,
         w_ff,
     )
     scratch = [
         pltpu.VMEM((S, D), BF16),
-        pltpu.VMEM((D, D), BF16),
+        pltpu.VMEM((D, 2 * HD + 2 * LANES), BF16),
         pltpu.VMEM((3, D, U), BF16),
         pltpu.VMEM((8, T), jnp.int32),
         pltpu.VMEM((8, D), F32),
         pltpu.VMEM((8, HD), F32),
         pltpu.VMEM((T, D), BF16),
         pltpu.VMEM((T, HD), F32),
-        pltpu.VMEM((T, HD), F32),
+        pltpu.VMEM((4, T, LANES), BF16),
         pltpu.VMEM((T, HD), BF16),
         pltpu.VMEM((2 * T, 2 * HD), BF16),
         pltpu.VMEM((T, 2 * T), F32),
@@ -864,7 +969,8 @@
         pltpu.VMEM((2, S, 2 * HD), BF16),
         pltpu.VMEM((S, 2 * HD), BF16),
         pltpu.VMEM((S, 2 * HD), BF16),
-        pltpu.VMEM((2, 2, S, 2 * HD), BF16),
+        pltpu.VMEM((4, S, LANES), BF16),
+        pltpu.VMEM((4, S, LANES), BF16),
         pltpu.VMEM((3, C * R, U), BF16),
         pltpu.VMEM((C - 1, 3, R, U), BF16),
         pltpu.VMEM((D, 2 * HD + LANES), BF16),
@@ -880,7 +986,7 @@
         pltpu.VMEM((2, 2, S, D), BF16),
         pltpu.SemaphoreType.DMA((SEMAPHORES,)),
         pltpu.SemaphoreType.DMA((SEMAPHORES,)),
-        pltpu.SemaphoreType.DMA((6,)),
+        pltpu.SemaphoreType.DMA((10,)),
     ]
     vmem = pl.BlockSpec(memory_space=pltpu.VMEM)
     anywhere = pl.BlockSpec(memory_space=pl.ANY)
@@ -896,7 +1002,7 @@
     block_out, input_grad, gain_sums, ff_grads, attn_grads, kv_grads = pl.pallas_call(
         functools.partial(fused_kernel, sizes),
         out_shape=results,
-        in_specs=[vmem] * 5 + [anywhere] * 3,
+        in_specs=[vmem] * 5 + [anywhere] * 6,
         out_specs=[anywhere] * 2 + [vmem, anywhere, vmem, vmem],
         scratch_shapes=scratch,
         compiler_params=pltpu.CompilerParams(

time: 376 us -> 327 us (0.87)
  Pallas kernels: 343 us -> 294 us
    pallas_call x1, Pallas kernels: 343 us -> 294 us  [fused(): pl.pallas_call(functools.partial(fused_kernel, sizes), out_shape=results,...]
where the time goes in v3:
time: 327 us; the launch traced here: 326 us
  Pallas kernels  294 us (90%)
  local copies, waits for them, and re-layouts  26.5 us (8%)
  other arithmetic  5.53 us (2%)
    pallas_call x1, Pallas kernels, fused(): pl.pallas_call(functools.partial(fused_kernel, sizes), out_shape=results,...  294 us
    unnamed x11, local copies, waits for them, and re-layouts  7.16 us

profile of v3, /device:TPU:0, one launch (start us, length us, event | category | flops | bytes accessed | tf_op | source)
XLA Modules:
  0.0 326.4 jit_solution(53902283058802800)
XLA Ops:
  0.6 0.0 copy-start.2
  0.7 0.1 pad.14.clone
  0.8 0.8 convert_element_type.14
  1.5 0.7 copy.25
  2.3 1.3 broadcast_in_dim.16.seg_row
  3.5 0.8 copy.24
  4.4 0.7 fusion.6.gain_cols
  5.1 1.5 copy.29.seg_col
  6.6 1.8 multiply_sine_fusion
  8.4 1.8 copy.26
  10.2 0.0 copy-done.2
  10.2 2.3 fusion.2
  12.5 2.5 reshape.50
  15.0 2.7 copy.39
  17.7 293.6 %shard_map.178 = (bf16[2,2,128,1152]{3,2,1,0:T(8,128)(2,1)}, bf16[2,2,128,1152]{3,2,1,0:T(8,128)(2,1)}, f32[8,1152]{1,0:T(8,128)}, f32[3,2,144,896]{3,2,1,0:T(8,...) custom-call(bf16[512,1152]{1,0:T(8,128)(2,1)} %bitcast.30, f32[512,128]{1,0:T(8,128)} %get-tuple-element.42.cosine, ...), custom_call_target="tpu_custom_call" | custom-call | tf_op jit(solution)/shard_map/pallas_call | solution.py:1002
  311.4 1.3 constant_dynamic-slice_fusion
  312.7 1.4 constant_dynamic-slice_fusion.1
  314.1 1.7 copy_bitcast_fusion.1
  315.8 1.7 fusion.7
  317.5 2.1 copy.36
  319.6 1.0 slice_bitcast_fusion
  320.6 0.1 slice.19
  320.7 0.0 copy-start.1
  320.7 2.9 copy.32
  323.6 0.0 copy-done.1
  323.6 0.0 copy-start
  323.6 1.0 copy.42
  324.7 0.7 copy-done
  325.3 1.0 copy.43
  (2 shorter events, 0.0 us)
Async XLA Ops:
  0.6 9.6 %copy-start.2 = (bf16[144,2,1728]{2,1,0:T(2,128)(2,1)S(1)}, bf16[144,2,1728]{2,1,0:T(2,128)(2,1)}, u32[]{:S(2)}) copy-start(bf16[144,2,1728]{2,1,0:T(2,128)(2,1)} %param.19) | copy-start | bytes 2985988
  320.7 2.9 copy-start.1
  323.6 1.7 copy-start

commit v4 on v3

--- a/solution.py
+++ b/solution.py
@@ -1,4 +1,5 @@
 import functools
+import math
 
 import jax
 import jax.numpy as jnp
@@ -60,7 +61,7 @@
 F32 = jnp.float32
 BF16 = jnp.bfloat16
 LANES = 128
-SEMAPHORES = 160
+SEMAPHORES = 171
 
 
 def mm(left, right):
@@ -90,25 +91,49 @@
     return jnp.concatenate([first * cosine + second * sine, second * cosine - first * sine], axis=1)
 
 
+def emit_kernel(count, *refs):
+    sources, results, held = refs[:count], refs[count : 2 * count], refs[2 * count : 3 * count]
+    incoming, outgoing = refs[3 * count :]
+    reads = [pltpu.make_async_copy(sources[n], held[n], incoming.at[n]) for n in range(count)]
+    writes = [pltpu.make_async_copy(held[n], results[n], outgoing.at[n]) for n in range(count)]
+    for moved in reads:
+        moved.start()
+    for n in range(count):
+        reads[n].wait()
+        writes[n].start()
+    for moved in writes:
+        moved.wait()
+
+
 def fused_kernel(
     sizes,
     act,
+    positions,
+    seg_ids,
+    norm_gains,
+    head_gains,
+    w_gateup,
+    w_down,
+    cot_all,
+    w_query,
+    w_keyval,
+    w_out,
+    out_block,
+    out_input,
+    out_norm,
+    out_head,
+    out_query,
+    out_kv,
+    out_out,
+    out_gateup,
+    out_down,
     cosine,
     sine,
     seg_row,
     seg_col,
-    cot_all,
-    w_query,
-    w_keyval,
-    w_out,
+    gain_pack,
     gain_cols,
     w_ff,
-    out_block,
-    out_input,
-    out_gains,
-    out_ff,
-    out_attn,
-    out_kv,
     cot,
     wa,
     wf,
@@ -163,12 +188,19 @@
     gain_z,
     block_all,
     input_all,
+    st_out,
+    st_query,
+    st_norm,
+    st_head,
+    st_kv,
     ss,
     rs,
     ls,
 ):
     C = sizes["context"]
     T, D, R, U = sizes["tokens"], sizes["width"], sizes["rows"], sizes["units"]
+    units = w_down.shape[1]
+    narrow = HD // (2 * C)
     S = T // 4
     f = lax.axis_index("fsdp")
     c = lax.axis_index("context")
@@ -227,6 +259,11 @@
     greeted += [{"context": base + 1 - m, "tensor": (1 - y) * 2 + core}]
     for device in greeted:
         pl.semaphore_signal(barrier, inc=1, device_id=device, device_id_type=MESH)
+    gain_pack[...] = jnp.zeros(gain_pack.shape, F32)
+    gain_pack[0:4, 0:R] = norm_gains[...].astype(F32)
+    gain_pack[4:6, 0:narrow] = head_gains[...].astype(F32)
+    gain_cols[...] = jnp.transpose(gain_pack[...])[0:R].astype(BF16)
+    seg_row[...] = jnp.broadcast_to(seg_ids[...], seg_row.shape)
     pl.semaphore_wait(barrier, len(greeted))
 
     mine = rows_of(f, c)
@@ -243,7 +280,7 @@
         local.append(pltpu.make_async_copy(part, wa.at[mine, cols], ls.at[6 + n]))
         local[-1].start()
     ka = slots(4 * C)
-    kar = slots(C)
+    kar = slots(C - 1)
     for step in range(1, C):
         for n, (part, cols) in enumerate(attn_parts):
             send(ka + 4 * step + n, part, wa.at[mine, cols], along(step))
@@ -255,33 +292,44 @@
     def _():
         copy(ks, seg_row, seg_left, {"context": c + 1}).start()
 
-    kf = slots(6 * C)
-
-    def send_ff(w):
-        k = kf + 2 * C * w
+    pieces = ((0, 0, 512), (0, 512, U), (1, 0, 512), (1, 512, U), (2, 0, 512), (2, 512, U))
+    kf = slots((2 * C - 1) * len(pieces))
+
+    def piece(p, rows):
+        w, low, high = pieces[p]
+        return wf.at[w, rows, low:high]
+
+    def send_ff(p):
+        k = kf + (2 * C - 1) * p
+        w, low, high = pieces[p]
         for step in range(1, C):
-            send(k + step, w_ff.at[(c + step) % 2, w], wf.at[w, mine], along(step))
-        send(k, w_ff.at[m, w], wf.at[w, mine], across)
-
-    def relay_ff(w, step):
-        k = kf + 2 * C * w
-        part = wf.at[w, rows_of(f, (c - step + C) % C)]
-        arrive(k + step, part)
-        copy(k + C + step, part, part, across).start()
-
-    def meet_ff(w):
-        k = kf + 2 * C * w
-        arrive(k, wf.at[w, rows_of(1 - f, c)])
+            send(k + step, w_ff.at[(c + step) % 2, w, :, low:high], piece(p, mine), along(step))
+        send(k, w_ff.at[m, w, :, low:high], piece(p, mine), across)
+
+    def relay_ff(p):
+        k = kf + (2 * C - 1) * p
         for step in range(1, C):
-            arrive(k + C + step, wf.at[w, rows_of(1 - f, (c - step + C) % C)])
-
-    def settle_ff(w):
-        k = kf + 2 * C * w
+            part = piece(p, rows_of(f, (c - step + C) % C))
+            arrive(k + step, part)
+            send(k + C - 1 + step, part, part, across)
+
+    def meet_ff(p):
+        k = kf + (2 * C - 1) * p
+        arrive(k, piece(p, rows_of(1 - f, c)))
         for step in range(1, C):
-            part = wf.at[w, rows_of(f, (c - step + C) % C)]
-            copy(k + C + step, part, part, across).wait_send()
-
-    send_ff(0)
+            arrive(k + C - 1 + step, piece(p, rows_of(1 - f, (c - step + C) % C)))
+
+    for w in range(3):
+        whole = w_down[...] if w == 2 else w_gateup[:, w, :]
+        w_ff[0, w] = whole[:, 0:U]
+        w_ff[1, w, :, 0 : units - U] = whole[:, U:units]
+        w_ff[1, w, :, units - U :] = jnp.zeros((R, 2 * U - units), BF16)
+    seg_col[...] = jnp.transpose(seg_row[...].astype(F32))[:, 0:1].astype(jnp.int32)
+    place = jnp.broadcast_to(positions[...].astype(F32), (8, T))
+    index = lax.broadcasted_iota(jnp.int32, (1, HD // 2), 1).astype(F32)
+    angle = jnp.transpose(place)[:, 0:1] * jnp.exp(index * (-2.0 * math.log(10000.0) / HD))
+    cosine[...] = jnp.cos(angle)
+    sine[...] = jnp.sin(angle)
     shard = pl.ds(pl.multiple_of(t * S, S), S)
     own_cot = pltpu.make_async_copy(cot_all.at[shard], cot, ls.at[2])
     own_cot.start()
@@ -291,13 +339,14 @@
         other = rows_of(f, (c - step + C) % C)
         for n, (_, cols) in enumerate(attn_parts):
             arrive(ka + 4 * step + n, wa.at[other, cols])
-        send(kar + step, wa.at[other], wa.at[other], across)
+        send(kar + step - 1, wa.at[other], wa.at[other], across)
     for moved in local:
         moved.wait()
+    send_ff(0)
     for n, (_, cols) in enumerate(attn_parts):
         arrive(ka + n, wa.at[rows_of(1 - f, c), cols])
     for step in range(1, C):
-        arrive(kar + step, wa.at[rows_of(1 - f, (c - step + C) % C)])
+        arrive(kar + step - 1, wa.at[rows_of(1 - f, (c - step + C) % C)])
 
     @pl.when(c > 0)
     def _():
@@ -310,7 +359,6 @@
 
     gain_t = jnp.transpose(wa[:, 2 * HD + LANES :].astype(F32))
     gain_rows[...] = gain_t[0:8]
-    narrow = HD // (2 * C)
     here = lax.broadcasted_iota(jnp.int32, (D, HD), 0)
     want = lax.broadcasted_iota(jnp.int32, (D, HD), 1)
     shift = narrow.bit_length() - 1
@@ -374,8 +422,8 @@
         copy(kk, kv.at[own_half], kv.at[my_half], {"context": c + 1}).start()
 
     send_ff(1)
-    for step in range(1, C):
-        relay_ff(0, step)
+    send_ff(2)
+    relay_ff(0)
 
     @pl.when(c > 0)
     def _():
@@ -437,8 +485,7 @@
         )
 
     kc = sum4(k4)
-    relay_ff(1, 1)
-    relay_ff(1, 2)
+    relay_ff(1)
     branch = finish4(kc)
     copy(kc, p4_sum, p4_chip, chip_of(1 - y, 2)).wait_send()
     for i in range(2):
@@ -497,27 +544,39 @@
             copy(ko + 4 + i, p8_sum.at[0], p8_chip.at[0], partner).wait_send()
         return total
 
-    kx = gather8(xg, low)
-    send_ff(2)
-    relay_ff(1, 3)
+    kx = slots(7)
+    beside, beyond = m * 2 + 1 - y, (1 - m) * 2 + y
+    corner = (1 - m) * 2 + 1 - y
+    xg[me, core] = low
+    send(kx + 2, xg.at[me, core], xg.at[me, core], chip_of(beyond, 4))
+    send(kx + 1, xg.at[me, core], xg.at[me, core], chip_of(beside, 4))
+    send(kx, xg.at[me, core], xg.at[me, core], partner)
+    send_ff(3)
+    send_ff(4)
+    relay_ff(2)
+    for i, k in ((1, beside), (2, beyond), (3, corner)):
+        part = xg.at[k, core]
+        arrive(kx + i, part)
+        if i == 2:
+            send(kx + 3, part, part, chip_of(beside, 4))
+        send(kx + 3 + i, part, part, partner)
+    send_ff(5)
+    relay_ff(3)
     own_ff.wait()
     own_cot.wait()
-    meet_ff(0)
-    meet_ff(1)
+    for p in range(4):
+        meet_ff(p)
+    arrive(kx, xg.at[me, 1 - core])
+    for i, k in ((1, beside), (2, beyond), (3, corner)):
+        arrive(kx + 3 + i, xg.at[k, 1 - core])
     root = 0.7978845608028654
     ko = slots(8)
 
     def forward(i, _):
         k = (me - i + 4) % 4
-        meet8(kx, xg, i)
         x = xg[k].reshape(2 * S, D)
         gate = mm(x, wf[0])
         up = mm(x, wf[1])
-
-        @pl.when(i < 3)
-        def _():
-            pass8(kx, xg, i + 1)
-
         square = gate * gate
         bent = jnp.tanh(root * gate * (1.0 + 0.044715 * square))
         ramp = 0.5 * (1.0 + bent)
@@ -526,15 +585,14 @@
         gel[k] = gelu.astype(BF16)
         upg[k] = (up * slope).astype(BF16)
         active[k] = (gelu * up).astype(BF16)
-
-        @pl.when(i > 0)
-        def _():
-            relay_ff(2, i)
-
         return 0
 
-    lax.fori_loop(0, 4, forward, 0)
-    meet_ff(2)
+    lax.fori_loop(0, 2, forward, 0)
+    relay_ff(4)
+    lax.fori_loop(2, 4, forward, 0)
+    relay_ff(5)
+    meet_ff(4)
+    meet_ff(5)
 
     def lower(i, _):
         k = (me - i + 4) % 4
@@ -549,7 +607,6 @@
 
     lax.fori_loop(0, 4, lower, 0)
     push8(ko, 3)
-    settle8(kx, xg)
     down = finish8(ko)
 
     factor = rms_factor(down)
@@ -606,22 +663,32 @@
     settle8(kd, dd)
 
     settle()
-    for w in range(3):
-        settle_ff(w)
     gall = wf
     mine_x = pl.ds(pl.multiple_of(f * C * R, C * R), C * R)
     theirs_x = pl.ds(pl.multiple_of((1 - f) * C * R, C * R), C * R)
+    ff_chunk = lambda w, low, high: (
+        gall.at[w, :, low:high],
+        gall_x.at[w, :, low:high],
+        gall_z.at[:, w, :, low:high],
+    )
+    attn_chunk = lambda low, high: (
+        ga.at[:, low:high],
+        ga_x.at[:, low:high],
+        ga_z.at[:, :, low:high],
+    )
     chunks = (
-        (2, 0, 256),
-        (2, 256, 512),
-        (2, 512, U),
-        (0, 0, 512),
-        (0, 512, U),
-        (1, 0, 512),
-        (1, 512, U),
+        ff_chunk(2, 0, 256),
+        ff_chunk(2, 256, 512),
+        ff_chunk(2, 512, U),
+        ff_chunk(0, 0, 512),
+        ff_chunk(0, 512, U),
+        attn_chunk(0, HD),
+        ff_chunk(1, 0, 640),
+        attn_chunk(HD, 2 * HD + LANES),
+        ff_chunk(1, 640, U),
     )
     kw = slots(len(chunks))
-    kz = slots(len(chunks) * C)
+    kz = slots(len(chunks) * (C - 1))
 
     def weight_grad(w, left, right, early):
         def tile(n, _):
@@ -637,35 +704,34 @@
         lax.fori_loop(0, first, lambda n, _: tile(n + (first + 1) * f, _), 0)
 
     def weight_send(q):
-        w, low, high = chunks[q]
-        send(kw + q, gall.at[w, theirs_x, low:high], gall_x.at[w, :, low:high], across)
+        full, from_x, _ = chunks[q]
+        send(kw + q, full.at[theirs_x], from_x, across)
 
     def weight_push(q):
-        w, low, high = chunks[q]
-        arrive(kw + q, gall_x.at[w, :, low:high])
+        full, from_x, from_z = chunks[q]
+        arrive(kw + q, from_x)
 
         def add(n, _):
             rows = pl.ds(pl.multiple_of(f * C * R + n * R, R), R)
             part = pl.ds(pl.multiple_of(n * R, R), R)
-            gall[w, rows, low:high] = (
-                gall[w, rows, low:high].astype(F32) + gall_x[w, part, low:high].astype(F32)
-            ).astype(BF16)
+            full[rows] = (full[rows].astype(F32) + from_x[part].astype(F32)).astype(BF16)
             return 0
 
         lax.fori_loop(0, C, add, 0)
         for step in range(1, C):
             send(
-                kz + q * C + step,
-                gall.at[w, rows_of(f, (c + step) % C), low:high],
-                gall_z.at[step - 1, w, :, low:high],
+                kz + q * (C - 1) + step - 1,
+                full.at[rows_of(f, (c + step) % C)],
+                from_z.at[step - 1],
                 along(step),
             )
 
+    def weight_meet(*which):
+        for q in which:
+            for step in range(1, C):
+                arrive(kz + q * (C - 1) + step - 1, chunks[q][2].at[step - 1])
+
     def weight_end(w):
-        for q, (chunk, low, high) in enumerate(chunks):
-            for step in range(1, C):
-                if chunk == w:
-                    arrive(kz + q * C + step, gall_z.at[step - 1, w, :, low:high])
         same = gall[w, rows_of(f, c)].astype(F32)
         other = jnp.zeros((R, U), F32)
         for step in range(1, C):
@@ -673,13 +739,16 @@
                 other = other + gall_z[step - 1, w].astype(F32)
             else:
                 same = same + gall_z[step - 1, w].astype(F32)
-        ff_stage[m] = same
-        ff_stage[1 - m] = other
-        saved = pltpu.make_async_copy(ff_stage, out_ff.at[w], ls.at[5])
+        ff_stage[:, 0:U] = jnp.where(m == 0, same, other)
+        ff_stage[:, U:units] = jnp.where(m == 0, other, same)[:, 0 : units - U]
+        into = out_down if w == 2 else out_gateup.at[:, w]
+        saved = pltpu.make_async_copy(ff_stage, into, ls.at[5])
         saved.start()
         saved.wait()
 
     weight_grad(2, dd, active, (0, 1, 2))
+    weight_grad(0, xg, upg, (3, 4))
+    weight_push(0)
     d_normed = finish8(ko2)
     hidden = hid[...]
     d_hidden, gain_2 = rms_backward(d_normed, hidden, rms_factor(hidden), gain(2))
@@ -691,11 +760,21 @@
     gain_mine[1:2] = gain_1
     db[y, core] = d_branch.astype(BF16)
     kb = share4(db)
-    weight_grad(0, xg, upg, (3, 4))
-    weight_push(0)
-    weight_grad(1, xg, gel, (5,))
     weight_push(1)
+    weight_grad(1, xg, gel, ())
+    weight_push(2)
     meet4(kb, db)
+
+    def out_grad(n, _):
+        cols = pl.ds(pl.multiple_of(n * LANES, LANES), LANES)
+        ga[cols, 0:HD] = contract_first(
+            db[:, :, :, cols].reshape(T, LANES), mix[...]
+        ).astype(BF16)
+        return 0
+
+    lax.fori_loop(0, D // LANES, out_grad, 0)
+    weight_send(5)
+    weight_send(6)
 
     def scores_back(i, gain_q):
         rows = pl.ds(pl.multiple_of(i * half, half), half)
@@ -731,10 +810,11 @@
     for i in range(2):
         send(kp + i, kvp.at[i, 1 - core], kvp_core.at[i], partner)
 
-    weight_push(2)
     arrive(kp + (1 - y), kvp_core.at[1 - y])
     kvp_sum[...] = (kvp[1 - y, core].astype(F32) + kvp_core[1 - y].astype(F32)).astype(BF16)
     send(kp + 2, kvp_sum, kvp_chip, chip_of(1 - y, 2))
+    kr = share4(block_all)
+    weight_push(3)
     arrive(kp + y, kvp_core.at[y])
     arrive(kp + 2, kvp_chip)
     d_left = (
@@ -747,7 +827,8 @@
     def _():
         copy(kt, ret_out, ret_in, {"context": c - 1}).start()
 
-    weight_push(3)
+    weight_push(4)
+    weight_push(5)
 
     @pl.when(c < C - 1)
     def _():
@@ -796,19 +877,17 @@
     def attn_grad(n, _):
         cols = pl.ds(pl.multiple_of(n * LANES, LANES), LANES)
         left = nrm[:, cols]
-        ga[cols, 0:HD] = contract_first(
-            db[:, :, :, cols].reshape(T, LANES), mix[...]
-        ).astype(BF16)
         ga[cols, HD : 2 * HD] = contract_first(left, dq[...]).astype(BF16)
         ga[cols, 2 * HD :] = contract_first(left, dkv_cols[...].reshape(T, LANES)).astype(BF16)
         return 0
 
     lax.fori_loop(0, D // LANES, attn_grad, 0)
-    ke = slots(1 + C)
-    send(ke, ga.at[theirs_x], ga_x, across)
-    weight_send(6)
+    weight_send(7)
+    weight_send(8)
     kc = sum4(k4)
-    weight_push(4)
+    meet4(kr, block_all)
+    save_block = pltpu.make_async_copy(block_all, out_block, ls.at[3])
+    save_block.start()
     d_normed = finish4(kc)
     copy(kc, p4_sum, p4_chip, chip_of(1 - y, 2)).wait_send()
     for i in range(2):
@@ -816,8 +895,6 @@
     values = act[shard].astype(F32)
     d_input, gain_0 = rms_backward(d_normed, values, rms_factor(values), gain(0))
     input_all[y, core] = (dhid[...] + d_input).astype(BF16)
-    ki = share4(input_all)
-    kr = share4(block_all)
     gain_mine[0:1] = gain_0
     gain_mine[4:8] = jnp.zeros((4, D), F32)
     gain_mine[4:5, 0:HD] = gain_q
@@ -825,50 +902,67 @@
     kn = slots(4 + 1 + C)
     for i in range(1, 4):
         send(kn + i, gain_mine, gain_tensor.at[i], {"tensor": (t + i) % 4})
-    weight_push(5)
+    ki = share4(input_all)
+    weight_push(6)
     total = gain_mine[...]
     for i in range(1, 4):
         arrive(kn + i, gain_tensor.at[i])
         total = total + gain_tensor[i]
     gain_tensor[0] = total
     send(kn, gain_tensor.at[0], gain_x.at[0], across)
+    weight_meet(0, 1, 2)
+    weight_end(2)
+    weight_push(7)
+    weight_push(8)
     meet4(ki, input_all)
     save_input = pltpu.make_async_copy(input_all, out_input, ls.at[4])
     save_input.start()
-    meet4(kr, block_all)
-    save_block = pltpu.make_async_copy(block_all, out_block, ls.at[3])
-    save_block.start()
-    arrive(ke, ga_x)
-    ga[mine_x] = (ga[mine_x].astype(F32) + ga_x[...].astype(F32)).astype(BF16)
-    for step in range(1, C):
-        send(ke + step, ga.at[rows_of(f, (c + step) % C)], ga_z.at[step - 1], along(step))
-    weight_push(6)
     arrive(kn, gain_x.at[0])
     gain_x[1] = total + gain_x[0]
     for step in range(1, C):
         send(kn + 4 + step, gain_x.at[1], gain_z.at[step], along(step))
-    weight_end(2)
+    weight_meet(3, 4)
     weight_end(0)
+    weight_meet(5, 7)
     attn = ga[rows_of(f, c)].astype(F32)
     for step in range(1, C):
-        arrive(ke + step, ga_z.at[step - 1])
         attn = attn + ga_z[step - 1].astype(F32)
-    out_attn[...] = attn[:, 0 : 2 * HD]
     kvg[t] = attn[:, 2 * HD :]
     kh = slots(4)
     for i in range(1, 4):
         send(kh + i, kvg.at[t], kvg.at[t], {"tensor": (t + i) % 4})
-    weight_end(1)
+    st_out[...] = attn[:, 0:HD]
+    st_query[...] = attn[:, HD : 2 * HD]
+    staged = []
+
+    def save(n, src, dst):
+        staged.append(pltpu.make_async_copy(src, dst, ls.at[10 + n]))
+        staged[-1].start()
+
+    save(0, st_out, out_out)
+    save(1, st_query, out_query)
     total = gain_x[1]
     for step in range(1, C):
         arrive(kn + 4 + step, gain_z.at[step])
         total = total + gain_z[step]
-    out_gains[...] = total
+    owner = f * C + c
+    moved = pltpu.roll(total, (D - owner * R) % D, 1)
+    st_norm[...] = moved[0:4, 0:R]
+    moved = pltpu.roll(total[:, 0:HD], (HD - owner * narrow) % HD, 1)
+    st_head[...] = moved[4:6, 0:narrow]
+    save(2, st_norm, out_norm)
+    save(3, st_head, out_head)
+    weight_meet(6, 8)
+    weight_end(1)
     for i in range(1, 4):
         arrive(kh + i, kvg.at[(t - i + 4) % 4])
-    out_kv[...] = kvg[...]
+    for k in range(4):
+        st_kv[:, k * LANES : (k + 1) * LANES] = kvg[k]
+    save(4, st_kv, out_kv)
     save_block.wait()
     save_input.wait()
+    for moved in staged:
+        moved.wait()
     settle()
 
     @pl.when(c < C - 1)
@@ -900,36 +994,28 @@
     R, units = w_down.shape
     U = -(-units // (2 * LANES)) * LANES
     S = T // 4
-    narrow = head_gains.shape[1]
-    gains = jnp.concatenate(
-        [
-            norm_gains.T,
-            jnp.pad(head_gains.T, ((0, R - narrow), (0, 0))),
-            jnp.zeros((R, LANES - 6), BF16),
-        ],
-        axis=1,
-    )
-    both = jnp.concatenate([w_gateup, w_down[:, None]], axis=1)
-    both = jnp.pad(both, ((0, 0), (0, 0), (0, 2 * U - units)))
-    w_ff = both.reshape(R, 3, 2, U).transpose(2, 1, 0, 3)
-    freqs = jnp.power(10000.0, -jnp.arange(HD // 2, dtype=F32) * 2.0 / HD)
-    angles = positions[0].astype(F32)[:, None] * freqs[None, :]
-    seg_row = jnp.broadcast_to(seg_ids, (8, T))
-    seg_col = seg_ids[0][:, None]
+    pack = -(-R // LANES) * LANES
     operands = (
         activations[0],
-        jnp.cos(angles),
-        jnp.sin(angles),
-        seg_row,
-        seg_col,
+        positions,
+        seg_ids,
+        norm_gains,
+        head_gains,
+        w_gateup,
+        w_down,
         cotangent[0],
         w_query,
         w_keyval,
         w_out,
-        gains,
-        w_ff,
     )
     scratch = [
+        pltpu.VMEM((T, HD // 2), F32),
+        pltpu.VMEM((T, HD // 2), F32),
+        pltpu.VMEM((8, T), jnp.int32),
+        pltpu.VMEM((T, 1), jnp.int32),
+        pltpu.VMEM((LANES, pack), F32),
+        pltpu.VMEM((R, LANES), BF16),
+        pltpu.VMEM((2, 3, R, U), BF16),
         pltpu.VMEM((S, D), BF16),
         pltpu.VMEM((D, 2 * HD + 2 * LANES), BF16),
         pltpu.VMEM((3, D, U), BF16),
@@ -977,53 +1063,56 @@
         pltpu.VMEM((C * R, 2 * HD + LANES), BF16),
         pltpu.VMEM((C - 1, R, 2 * HD + LANES), BF16),
         pltpu.VMEM((4, R, LANES), F32),
-        pltpu.VMEM((2, R, U), F32),
+        pltpu.VMEM((R, units), F32),
         pltpu.VMEM((8, D), F32),
         pltpu.VMEM((4, 8, D), F32),
         pltpu.VMEM((2, 8, D), F32),
         pltpu.VMEM((C, 8, D), F32),
         pltpu.VMEM((2, 2, S, D), BF16),
         pltpu.VMEM((2, 2, S, D), BF16),
+        pltpu.VMEM((R, HD), F32),
+        pltpu.VMEM((R, HD), F32),
+        pltpu.VMEM(norm_gains.shape, F32),
+        pltpu.VMEM(head_gains.shape, F32),
+        pltpu.VMEM((R, 2 * HD), F32),
         pltpu.SemaphoreType.DMA((SEMAPHORES,)),
         pltpu.SemaphoreType.DMA((SEMAPHORES,)),
-        pltpu.SemaphoreType.DMA((10,)),
+        pltpu.SemaphoreType.DMA((15,)),
     ]
     vmem = pl.BlockSpec(memory_space=pltpu.VMEM)
     anywhere = pl.BlockSpec(memory_space=pl.ANY)
     results = (
         jax.ShapeDtypeStruct((2, 2, S, D), BF16),
         jax.ShapeDtypeStruct((2, 2, S, D), BF16),
-        jax.ShapeDtypeStruct((8, D), F32),
-        jax.ShapeDtypeStruct((3, 2, R, U), F32),
-        jax.ShapeDtypeStruct((R, 2 * HD), F32),
-        jax.ShapeDtypeStruct((4, R, LANES), F32),
+        jax.ShapeDtypeStruct(norm_gains.shape, F32),
+        jax.ShapeDtypeStruct(head_gains.shape, F32),
+        jax.ShapeDtypeStruct(w_query.shape, F32),
+        jax.ShapeDtypeStruct(w_keyval.shape, F32),
+        jax.ShapeDtypeStruct(w_out.shape, F32),
+        jax.ShapeDtypeStruct(w_gateup.shape, F32),
+        jax.ShapeDtypeStruct(w_down.shape, F32),
     )
     sizes = {"context": C, "tokens": T, "width": D, "rows": R, "units": U}
-    block_out, input_grad, gain_sums, ff_grads, attn_grads, kv_grads = pl.pallas_call(
+    parts = pl.pallas_call(
         functools.partial(fused_kernel, sizes),
         out_shape=results,
-        in_specs=[vmem] * 5 + [anywhere] * 6,
-        out_specs=[anywhere] * 2 + [vmem, anywhere, vmem, vmem],
+        in_specs=[vmem] * 7 + [anywhere] * 4,
+        out_specs=[anywhere] * len(results),
         scratch_shapes=scratch,
         compiler_params=pltpu.CompilerParams(
             collective_id=0, has_side_effects=True, vmem_limit_bytes=67043328
         ),
     )(*operands)
-    owner = lax.axis_index(("fsdp", "context"))
-    norm_grad = lax.dynamic_slice(gain_sums, (0, owner * R), (4, R))
-    head_grad = lax.dynamic_slice(gain_sums, (4, owner * narrow), (2, narrow))
-    ff = ff_grads.transpose(2, 0, 1, 3).reshape(R, 3, 2 * U)[:, :, :units]
-    return (
-        block_out.reshape(1, T, D),
-        input_grad.reshape(1, T, D),
-        norm_grad,
-        head_grad,
-        attn_grads[:, HD:],
-        kv_grads.transpose(1, 0, 2).reshape(R, 2 * HD),
-        attn_grads[:, :HD],
-        ff[:, :2],
-        ff[:, 2],
-    )
+    count = len(parts)
+    block_out, input_grad, *grads = pl.pallas_call(
+        functools.partial(emit_kernel, count),
+        out_shape=results,
+        in_specs=[anywhere] * count,
+        out_specs=[anywhere] * count,
+        scratch_shapes=[pltpu.VMEM(part.shape, part.dtype) for part in parts]
+        + [pltpu.SemaphoreType.DMA((count,))] * 2,
+    )(*parts)
+    return block_out.reshape(1, T, D), input_grad.reshape(1, T, D), *grads
 
 
 def block(mesh, *arrays):

time: 327 us -> 279 us (0.85)
  local copies, waits for them, and re-layouts: 26.5 us -> 0 us
  Pallas kernels: 294 us -> 276 us
  other arithmetic: 5.53 us -> 0 us
    pallas_call x1, Pallas kernels: 294 us -> 271 us  [fused(): pl.pallas_call(functools.partial(fused_kernel, sizes), out_shape=results,...]
    reshape x4 -> x0, local copies, waits for them, and re-layouts: 9.01 us -> none  [the longest x2 5.22 us: fused(): w_ff = both.reshape(R, 3, 2, U).transpose(2, 1, 0, 3)]
    unnamed x11 -> x0, local copies, waits for them, and re-layouts: 7.16 us -> none
    pallas_call x0 -> x1, Pallas kernels: none -> 4.93 us  [fused(): pl.pallas_call(functools.partial(emit_kernel, count), out_shape=results,...]
where the time goes in v4:
time: 279 us; the launch traced here: 277 us
  Pallas kernels  276 us (99%)
    pallas_call x1, Pallas kernels, fused(): pl.pallas_call(functools.partial(fused_kernel, sizes), out_shape=results,...  271 us

profile of v4, /device:TPU:0, one launch (start us, length us, event | category | flops | bytes accessed | tf_op | source)
XLA Modules:
  0.0 276.5 jit_solution(9444573522236718193)
XLA Ops:
  0.6 270.8 %shard_map.178 = (bf16[2,2,128,1152]{3,2,1,0:T(8,128)(2,1)}, bf16[2,2,128,1152]{3,2,1,0:T(8,128)(2,1)}, f32[4,144]{1,0:T(4,128)}, f32[2,32]{1,0:T(2,128)}, f32[1...) custom-call(bf16[512,1152]{1,0:T(8,128)(2,1)} %bitcast.4, ...), custom_call_target="tpu_custom_call" | custom-call | tf_op jit(solution)/shard_map/pallas_call | solution.py:1096
  271.4 4.9 %shard_map.179 = (bf16[2,2,128,1152]{3,2,1,0:T(8,128)(2,1)}, bf16[2,2,128,1152]{3,2,1,0:T(8,128)(2,1)}, f32[4,144]{1,0:T(4,128)}, f32[2,32]{1,0:T(2,128)}, f32[1...) custom-call(bf16[2,2,128,1152]{3,2,1,0:T(8,128)(2,1)} %get-tuple-ele, ...), custom_call_target="tpu_custom_call" | custom-call | tf_op jit(solution)/shard_map/pallas_call | solution.py:1107

commit v5 on v4

--- a/solution.py
+++ b/solution.py
@@ -61,7 +61,7 @@
 F32 = jnp.float32
 BF16 = jnp.bfloat16
 LANES = 128
-SEMAPHORES = 171
+SEMAPHORES = 174
 
 
 def mm(left, right):
@@ -132,7 +132,7 @@
     seg_row,
     seg_col,
     gain_pack,
-    gain_cols,
+    gain_all,
     w_ff,
     cot,
     wa,
@@ -262,7 +262,6 @@
     gain_pack[...] = jnp.zeros(gain_pack.shape, F32)
     gain_pack[0:4, 0:R] = norm_gains[...].astype(F32)
     gain_pack[4:6, 0:narrow] = head_gains[...].astype(F32)
-    gain_cols[...] = jnp.transpose(gain_pack[...])[0:R].astype(BF16)
     seg_row[...] = jnp.broadcast_to(seg_ids[...], seg_row.shape)
     pl.semaphore_wait(barrier, len(greeted))
 
@@ -272,44 +271,59 @@
         (w_query, slice(0, HD)),
         (w_keyval.at[:, kv_cols], slice(HD, HD + LANES)),
         (w_out, slice(HD + LANES, 2 * HD + LANES)),
-        (gain_cols, slice(2 * HD + LANES, 2 * HD + 2 * LANES)),
     )
     q_cols, kv_part, o_cols = (cols for _, cols in attn_parts[:3])
     local = []
     for n, (part, cols) in enumerate(attn_parts):
         local.append(pltpu.make_async_copy(part, wa.at[mine, cols], ls.at[6 + n]))
         local[-1].start()
-    ka = slots(4 * C)
+    ka = slots(3 * C)
     kar = slots(C - 1)
+    kg = slots(2 * C - 1)
     for step in range(1, C):
         for n, (part, cols) in enumerate(attn_parts):
-            send(ka + 4 * step + n, part, wa.at[mine, cols], along(step))
+            send(ka + 3 * step + n, part, wa.at[mine, cols], along(step))
     for n, (part, cols) in enumerate(attn_parts):
         send(ka + n, part, wa.at[mine, cols], across)
+    own_gain = gain_all.at[f * C + c]
+    gain_all[f * C + c] = gain_pack[...]
+    for step in range(1, C):
+        send(kg + step, gain_pack, own_gain, along(step))
+    send(kg, gain_pack, own_gain, across)
     ks = slots(1)
 
     @pl.when(c < C - 1)
     def _():
         copy(ks, seg_row, seg_left, {"context": c + 1}).start()
 
-    pieces = ((0, 0, 512), (0, 512, U), (1, 0, 512), (1, 512, U), (2, 0, 512), (2, 512, U))
+    pieces = ((0, 0, 384), (0, 384, U), (1, 0, 512), (1, 512, U), (2, 0, 512), (2, 512, U))
     kf = slots((2 * C - 1) * len(pieces))
 
     def piece(p, rows):
         w, low, high = pieces[p]
         return wf.at[w, rows, low:high]
 
+    side = c // 2
+    near, far = 2 - side, 3 * (1 - side)
+
     def send_ff(p):
         k = kf + (2 * C - 1) * p
         w, low, high = pieces[p]
-        for step in range(1, C):
-            send(k + step, w_ff.at[(c + step) % 2, w, :, low:high], piece(p, mine), along(step))
+        turns = tuple((c + step) % C for step in range(1, C))
+        for to in (base + 1 - m, near, far) if p in (3, 4) else turns:
+            send(
+                k + (to - c + C) % C,
+                w_ff.at[to % 2, w, :, low:high],
+                piece(p, mine),
+                {"context": to},
+            )
         send(k, w_ff.at[m, w, :, low:high], piece(p, mine), across)
 
     def relay_ff(p):
         k = kf + (2 * C - 1) * p
-        for step in range(1, C):
-            part = piece(p, rows_of(f, (c - step + C) % C))
+        for source in (base + 1 - m, near, far):
+            step = (c - source + C) % C
+            part = piece(p, rows_of(f, source))
             arrive(k + step, part)
             send(k + C - 1 + step, part, part, across)
 
@@ -338,8 +352,11 @@
     for step in range(1, C):
         other = rows_of(f, (c - step + C) % C)
         for n, (_, cols) in enumerate(attn_parts):
-            arrive(ka + 4 * step + n, wa.at[other, cols])
+            arrive(ka + 3 * step + n, wa.at[other, cols])
         send(kar + step - 1, wa.at[other], wa.at[other], across)
+        part = gain_all.at[f * C + (c - step + C) % C]
+        arrive(kg + step, part)
+        send(kg + C - 1 + step, part, part, across)
     for moved in local:
         moved.wait()
     send_ff(0)
@@ -357,14 +374,18 @@
         seg_left[...] = jnp.full(seg_left.shape, -1, jnp.int32)
         kv[0:T] = jnp.zeros((T, 2 * HD), BF16)
 
-    gain_t = jnp.transpose(wa[:, 2 * HD + LANES :].astype(F32))
-    gain_rows[...] = gain_t[0:8]
-    here = lax.broadcasted_iota(jnp.int32, (D, HD), 0)
-    want = lax.broadcasted_iota(jnp.int32, (D, HD), 1)
-    shift = narrow.bit_length() - 1
-    want = lax.shift_right_logical(want, shift) * R + (want & (narrow - 1))
-    pick = jnp.where(here == want, 1.0, 0.0).astype(BF16)
-    head_rows[...] = mm(gain_t[0:16].astype(BF16), pick)[0:8]
+    arrive(kg, gain_all.at[(1 - f) * C + c])
+    for step in range(1, C):
+        arrive(kg + C - 1 + step, gain_all.at[(1 - f) * C + (c - step + C) % C])
+    wide = jnp.zeros((8, D), F32)
+    heads = jnp.zeros((8, HD), F32)
+    blank = jnp.zeros((8, D - gain_pack.shape[1]), F32)
+    for j in range(2 * C):
+        part = gain_all[j]
+        wide = wide + pltpu.roll(jnp.concatenate([part, blank], axis=1), j * R, 1)
+        heads = heads + pltpu.roll(part[:, 0:HD], j * narrow, 1)
+    gain_rows[...] = wide
+    head_rows[...] = heads
 
     def gain(index):
         return gain_rows[index : index + 1]
@@ -554,13 +575,13 @@
     send_ff(3)
     send_ff(4)
     relay_ff(2)
+    send_ff(5)
     for i, k in ((1, beside), (2, beyond), (3, corner)):
         part = xg.at[k, core]
         arrive(kx + i, part)
         if i == 2:
             send(kx + 3, part, part, chip_of(beside, 4))
         send(kx + 3 + i, part, part, partner)
-    send_ff(5)
     relay_ff(3)
     own_ff.wait()
     own_cot.wait()
@@ -690,18 +711,24 @@
     kw = slots(len(chunks))
     kz = slots(len(chunks) * (C - 1))
 
-    def weight_grad(w, left, right, early):
-        def tile(n, _):
+    def weight_grad(w, left, right, early, lead=0):
+        def tile(n, low, high):
             cols = pl.ds(pl.multiple_of(n * LANES, LANES), LANES)
             block = left[:, :, :, cols].reshape(8 * S, LANES)
-            gall[w, cols] = contract_first(block, right[...].reshape(8 * S, U)).astype(BF16)
+            gall[w, cols, low:high] = contract_first(
+                block, right[:, :, low:high].reshape(8 * S, high - low)
+            ).astype(BF16)
             return 0
 
         first = D // LANES // 2
-        lax.fori_loop(0, first + 1, lambda n, _: tile(n + first * (1 - f), _), 0)
+        if lead:
+            lax.fori_loop(0, first + 1, lambda n, _: tile(n + first * (1 - f), 0, lead), 0)
+            weight_send(early[0])
+            early = early[1:]
+        lax.fori_loop(0, first + 1, lambda n, _: tile(n + first * (1 - f), lead, U), 0)
         for q in early:
             weight_send(q)
-        lax.fori_loop(0, first, lambda n, _: tile(n + (first + 1) * f, _), 0)
+        lax.fori_loop(0, first, lambda n, _: tile(n + (first + 1) * f, 0, U), 0)
 
     def weight_send(q):
         full, from_x, _ = chunks[q]
@@ -718,12 +745,13 @@
             return 0
 
         lax.fori_loop(0, C, add, 0)
-        for step in range(1, C):
+        for to in (far, near, base + 1 - m):
+            step = (to - c + C) % C
             send(
                 kz + q * (C - 1) + step - 1,
-                full.at[rows_of(f, (c + step) % C)],
+                full.at[rows_of(f, to)],
                 from_z.at[step - 1],
-                along(step),
+                {"context": to},
             )
 
     def weight_meet(*which):
@@ -746,7 +774,7 @@
         saved.start()
         saved.wait()
 
-    weight_grad(2, dd, active, (0, 1, 2))
+    weight_grad(2, dd, active, (0, 1, 2), 256)
     weight_grad(0, xg, upg, (3, 4))
     weight_push(0)
     d_normed = finish8(ko2)
@@ -884,6 +912,7 @@
     lax.fori_loop(0, D // LANES, attn_grad, 0)
     weight_send(7)
     weight_send(8)
+    weight_push(6)
     kc = sum4(k4)
     meet4(kr, block_all)
     save_block = pltpu.make_async_copy(block_all, out_block, ls.at[3])
@@ -903,24 +932,23 @@
     for i in range(1, 4):
         send(kn + i, gain_mine, gain_tensor.at[i], {"tensor": (t + i) % 4})
     ki = share4(input_all)
-    weight_push(6)
+    weight_push(7)
     total = gain_mine[...]
     for i in range(1, 4):
         arrive(kn + i, gain_tensor.at[i])
         total = total + gain_tensor[i]
     gain_tensor[0] = total
     send(kn, gain_tensor.at[0], gain_x.at[0], across)
-    weight_meet(0, 1, 2)
-    weight_end(2)
-    weight_push(7)
     weight_push(8)
-    meet4(ki, input_all)
-    save_input = pltpu.make_async_copy(input_all, out_input, ls.at[4])
-    save_input.start()
     arrive(kn, gain_x.at[0])
     gain_x[1] = total + gain_x[0]
     for step in range(1, C):
         send(kn + 4 + step, gain_x.at[1], gain_z.at[step], along(step))
+    weight_meet(0, 1, 2)
+    weight_end(2)
+    meet4(ki, input_all)
+    save_input = pltpu.make_async_copy(input_all, out_input, ls.at[4])
+    save_input.start()
     weight_meet(3, 4)
     weight_end(0)
     weight_meet(5, 7)
@@ -973,6 +1001,7 @@
     @pl.when(c > 0)
     def _():
         copy(kt, ret_out, ret_in, {"context": c - 1}).wait_send()
+    assert counter[0] == SEMAPHORES, counter
 
 
 def fused(
@@ -1013,11 +1042,11 @@
         pltpu.VMEM((T, HD // 2), F32),
         pltpu.VMEM((8, T), jnp.int32),
         pltpu.VMEM((T, 1), jnp.int32),
-        pltpu.VMEM((LANES, pack), F32),
-        pltpu.VMEM((R, LANES), BF16),
+        pltpu.VMEM((8, pack), F32),
+        pltpu.VMEM((2 * C, 8, pack), F32),
         pltpu.VMEM((2, 3, R, U), BF16),
         pltpu.VMEM((S, D), BF16),
-        pltpu.VMEM((D, 2 * HD + 2 * LANES), BF16),
+        pltpu.VMEM((D, 2 * HD + LANES), BF16),
         pltpu.VMEM((3, D, U), BF16),
         pltpu.VMEM((8, T), jnp.int32),
         pltpu.VMEM((8, D), F32),

time: 279 us -> 277 us (level)
  the two profiles are of different devices: /device:TPU:0 before, /device:TPU:31 now
where the time goes in v5:
time: 277 us
  Pallas kernels  276 us (100%)
    pallas_call x1, Pallas kernels, fused(): pl.pallas_call(functools.partial(fused_kernel, sizes), out_shape=results,...  271 us

profile of v5, /device:TPU:31, one launch (start us, length us, event | category | flops | bytes accessed | tf_op | source)
XLA Modules:
  0.0 277.1 jit_solution(6385352123479592263)
XLA Ops:
  0.6 271.3 %shard_map.178 = (bf16[2,2,128,1152]{3,2,1,0:T(8,128)(2,1)}, bf16[2,2,128,1152]{3,2,1,0:T(8,128)(2,1)}, f32[4,144]{1,0:T(4,128)}, f32[2,32]{1,0:T(2,128)}, f32[1...) custom-call(bf16[512,1152]{1,0:T(8,128)(2,1)} %bitcast.4, ...), custom_call_target="tpu_custom_call" | custom-call | tf_op jit(solution)/shard_map/pallas_call | solution.py:1125
  271.9 4.9 %shard_map.179 = (bf16[2,2,128,1152]{3,2,1,0:T(8,128)(2,1)}, bf16[2,2,128,1152]{3,2,1,0:T(8,128)(2,1)}, f32[4,144]{1,0:T(4,128)}, f32[2,32]{1,0:T(2,128)}, f32[1...) custom-call(bf16[2,2,128,1152]{3,2,1,0:T(8,128)(2,1)} %get-tuple-ele, ...), custom_call_target="tpu_custom_call" | custom-call | tf_op jit(solution)/shard_map/pallas_call | solution.py:1136

commit v6 on v5

--- a/solution.py
+++ b/solution.py
@@ -61,7 +61,7 @@
 F32 = jnp.float32
 BF16 = jnp.bfloat16
 LANES = 128
-SEMAPHORES = 174
+SEMAPHORES = 178
 
 
 def mm(left, right):
@@ -576,13 +576,14 @@
     send_ff(4)
     relay_ff(2)
     send_ff(5)
+    relay_ff(3)
     for i, k in ((1, beside), (2, beyond), (3, corner)):
         part = xg.at[k, core]
         arrive(kx + i, part)
         if i == 2:
             send(kx + 3, part, part, chip_of(beside, 4))
         send(kx + 3 + i, part, part, partner)
-    relay_ff(3)
+    relay_ff(4)
     own_ff.wait()
     own_cot.wait()
     for p in range(4):
@@ -608,10 +609,9 @@
         active[k] = (gelu * up).astype(BF16)
         return 0
 
-    lax.fori_loop(0, 2, forward, 0)
-    relay_ff(4)
-    lax.fori_loop(2, 4, forward, 0)
+    lax.fori_loop(0, 3, forward, 0)
     relay_ff(5)
+    lax.fori_loop(3, 4, forward, 0)
     meet_ff(4)
     meet_ff(5)
 
@@ -698,13 +698,14 @@
         ga_z.at[:, :, low:high],
     )
     chunks = (
-        ff_chunk(2, 0, 256),
-        ff_chunk(2, 256, 512),
-        ff_chunk(2, 512, U),
+        ff_chunk(2, 0, 128),
+        ff_chunk(2, 128, 384),
+        ff_chunk(2, 384, U),
         ff_chunk(0, 0, 512),
         ff_chunk(0, 512, U),
         attn_chunk(0, HD),
-        ff_chunk(1, 0, 640),
+        ff_chunk(1, 0, 256),
+        ff_chunk(1, 256, 640),
         attn_chunk(HD, 2 * HD + LANES),
         ff_chunk(1, 640, U),
     )
@@ -774,9 +775,10 @@
         saved.start()
         saved.wait()
 
-    weight_grad(2, dd, active, (0, 1, 2), 256)
+    weight_grad(2, dd, active, (0, 1, 2), 128)
+    weight_push(0)
     weight_grad(0, xg, upg, (3, 4))
-    weight_push(0)
+    weight_push(1)
     d_normed = finish8(ko2)
     hidden = hid[...]
     d_hidden, gain_2 = rms_backward(d_normed, hidden, rms_factor(hidden), gain(2))
@@ -788,7 +790,6 @@
     gain_mine[1:2] = gain_1
     db[y, core] = d_branch.astype(BF16)
     kb = share4(db)
-    weight_push(1)
     weight_grad(1, xg, gel, ())
     weight_push(2)
     meet4(kb, db)
@@ -803,6 +804,7 @@
     lax.fori_loop(0, D // LANES, out_grad, 0)
     weight_send(5)
     weight_send(6)
+    weight_send(7)
 
     def scores_back(i, gain_q):
         rows = pl.ds(pl.multiple_of(i * half, half), half)
@@ -857,6 +859,7 @@
 
     weight_push(4)
     weight_push(5)
+    weight_push(6)
 
     @pl.when(c < C - 1)
     def _():
@@ -910,9 +913,9 @@
         return 0
 
     lax.fori_loop(0, D // LANES, attn_grad, 0)
-    weight_send(7)
     weight_send(8)
-    weight_push(6)
+    weight_send(9)
+    weight_push(7)
     kc = sum4(k4)
     meet4(kr, block_all)
     save_block = pltpu.make_async_copy(block_all, out_block, ls.at[3])
@@ -932,18 +935,18 @@
     for i in range(1, 4):
         send(kn + i, gain_mine, gain_tensor.at[i], {"tensor": (t + i) % 4})
     ki = share4(input_all)
-    weight_push(7)
+    weight_push(8)
     total = gain_mine[...]
     for i in range(1, 4):
         arrive(kn + i, gain_tensor.at[i])
         total = total + gain_tensor[i]
     gain_tensor[0] = total
     send(kn, gain_tensor.at[0], gain_x.at[0], across)
-    weight_push(8)
     arrive(kn, gain_x.at[0])
     gain_x[1] = total + gain_x[0]
     for step in range(1, C):
         send(kn + 4 + step, gain_x.at[1], gain_z.at[step], along(step))
+    weight_push(9)
     weight_meet(0, 1, 2)
     weight_end(2)
     meet4(ki, input_all)
@@ -951,7 +954,7 @@
     save_input.start()
     weight_meet(3, 4)
     weight_end(0)
-    weight_meet(5, 7)
+    weight_meet(5, 8)
     attn = ga[rows_of(f, c)].astype(F32)
     for step in range(1, C):
         attn = attn + ga_z[step - 1].astype(F32)
@@ -980,7 +983,7 @@
     st_head[...] = moved[4:6, 0:narrow]
     save(2, st_norm, out_norm)
     save(3, st_head, out_head)
-    weight_meet(6, 8)
+    weight_meet(6, 7, 9)
     weight_end(1)
     for i in range(1, 4):
         arrive(kh + i, kvg.at[(t - i + 4) % 4])

time: 277 us -> 275 us (level)
  the two profiles are of different devices: /device:TPU:31 before, /device:TPU:0 now
where the time goes in v6:
time: 275 us; the launch traced here: 274 us
  Pallas kernels  273 us (99%)
    pallas_call x1, Pallas kernels, fused(): pl.pallas_call(functools.partial(fused_kernel, sizes), out_shape=results,...  268 us

profile of v6, /device:TPU:0, one launch (start us, length us, event | category | flops | bytes accessed | tf_op | source)
XLA Modules:
  0.0 273.6 jit_solution(1939689107938509015)
XLA Ops:
  0.6 267.9 %shard_map.178 = (bf16[2,2,128,1152]{3,2,1,0:T(8,128)(2,1)}, bf16[2,2,128,1152]{3,2,1,0:T(8,128)(2,1)}, f32[4,144]{1,0:T(4,128)}, f32[2,32]{1,0:T(2,128)}, f32[1...) custom-call(bf16[512,1152]{1,0:T(8,128)(2,1)} %bitcast.4, ...), custom_call_target="tpu_custom_call" | custom-call | tf_op jit(solution)/shard_map/pallas_call | solution.py:1128
  268.5 4.9 %shard_map.179 = (bf16[2,2,128,1152]{3,2,1,0:T(8,128)(2,1)}, bf16[2,2,128,1152]{3,2,1,0:T(8,128)(2,1)}, f32[4,144]{1,0:T(4,128)}, f32[2,32]{1,0:T(2,128)}, f32[1...) custom-call(bf16[2,2,128,1152]{3,2,1,0:T(8,128)(2,1)} %get-tuple-ele, ...), custom_call_target="tpu_custom_call" | custom-call | tf_op jit(solution)/shard_map/pallas_call | solution.py:1139

commit v7 on v6

--- a/solution.py
+++ b/solution.py
@@ -107,13 +107,13 @@
 
 def fused_kernel(
     sizes,
-    act,
+    act_all,
     positions,
     seg_ids,
     norm_gains,
     head_gains,
-    w_gateup,
-    w_down,
+    gateup_all,
+    down_all,
     cot_all,
     w_query,
     w_keyval,
@@ -127,6 +127,9 @@
     out_out,
     out_gateup,
     out_down,
+    act,
+    w_gateup,
+    w_down,
     cosine,
     sine,
     seg_row,
@@ -253,6 +256,15 @@
             return {"tensor": k * 2 + core}
         return {"context": base + k // 2, "tensor": (k % 2) * 2 + core}
 
+    loads = [
+        pltpu.make_async_copy(src, dst, ls.at[15 + n])
+        for n, (src, dst) in enumerate(
+            ((gateup_all, w_gateup), (down_all, w_down), (act_all, act))
+        )
+    ]
+    for moved in loads:
+        moved.start()
+
     barrier = pltpu.get_barrier_semaphore()
     greeted = [along(step) for step in range(1, C)] + [across]
     greeted += [{"tensor": (t + step) % 4} for step in range(1, 4)]
@@ -333,6 +345,8 @@
         for step in range(1, C):
             arrive(k + C - 1 + step, piece(p, rows_of(1 - f, (c - step + C) % C)))
 
+    for moved in loads:
+        moved.wait()
     for w in range(3):
         whole = w_down[...] if w == 2 else w_gateup[:, w, :]
         w_ff[0, w] = whole[:, 0:U]
@@ -1041,6 +1055,9 @@
         w_out,
     )
     scratch = [
+        pltpu.VMEM((T, D), BF16),
+        pltpu.VMEM(w_gateup.shape, BF16),
+        pltpu.VMEM(w_down.shape, BF16),
         pltpu.VMEM((T, HD // 2), F32),
         pltpu.VMEM((T, HD // 2), F32),
         pltpu.VMEM((8, T), jnp.int32),
@@ -1109,7 +1126,7 @@
         pltpu.VMEM((R, 2 * HD), F32),
         pltpu.SemaphoreType.DMA((SEMAPHORES,)),
         pltpu.SemaphoreType.DMA((SEMAPHORES,)),
-        pltpu.SemaphoreType.DMA((15,)),
+        pltpu.SemaphoreType.DMA((18,)),
     ]
     vmem = pl.BlockSpec(memory_space=pltpu.VMEM)
     anywhere = pl.BlockSpec(memory_space=pl.ANY)
@@ -1128,7 +1145,7 @@
     parts = pl.pallas_call(
         functools.partial(fused_kernel, sizes),
         out_shape=results,
-        in_specs=[vmem] * 7 + [anywhere] * 4,
+        in_specs=[anywhere] + [vmem] * 4 + [anywhere] * 6,
         out_specs=[anywhere] * len(results),
         scratch_shapes=scratch,
         compiler_params=pltpu.CompilerParams(

time: 275 us -> 274 us (level)
  no operation moved by 1% of the time
where the time goes in v7:
time: 274 us; the launch traced here: 273 us
  Pallas kernels  272 us (99%)
    pallas_call x1, Pallas kernels, fused(): pl.pallas_call(functools.partial(fused_kernel, sizes), out_shape=results,...  267 us

profile of v7, /device:TPU:0, one launch (start us, length us, event | category | flops | bytes accessed | tf_op | source)
XLA Modules:
  0.0 272.7 jit_solution(15015640474115291033)
XLA Ops:
  0.6 266.9 %shard_map.178 = (bf16[2,2,128,1152]{3,2,1,0:T(8,128)(2,1)}, bf16[2,2,128,1152]{3,2,1,0:T(8,128)(2,1)}, f32[4,144]{1,0:T(4,128)}, f32[2,32]{1,0:T(2,128)}, f32[1...) custom-call(bf16[512,1152]{1,0:T(8,128)(2,1)} %bitcast.4, ...), custom_call_target="tpu_custom_call" | custom-call | tf_op jit(solution)/shard_map/pallas_call | solution.py:1145
  267.6 4.9 %shard_map.179 = (bf16[2,2,128,1152]{3,2,1,0:T(8,128)(2,1)}, bf16[2,2,128,1152]{3,2,1,0:T(8,128)(2,1)}, f32[4,144]{1,0:T(4,128)}, f32[2,32]{1,0:T(2,128)}, f32[1...) custom-call(bf16[2,2,128,1152]{3,2,1,0:T(8,128)(2,1)} %get-tuple-ele, ...), custom_call_target="tpu_custom_call" | custom-call | tf_op jit(solution)/shard_map/pallas_call | solution.py:1156

commit v8 on v7

--- a/solution.py
+++ b/solution.py
@@ -760,8 +760,8 @@
             return 0
 
         lax.fori_loop(0, C, add, 0)
-        for to in (far, near, base + 1 - m):
-            step = (to - c + C) % C
+        for step in range(1, C):
+            to = (c + step) % C
             send(
                 kz + q * (C - 1) + step - 1,
                 full.at[rows_of(f, to)],

time: 274 us -> 274 us (level)
  no operation moved by 1% of the time
where the time goes in v8:
time: 274 us; the launch traced here: 273 us
  Pallas kernels  272 us (99%)
    pallas_call x1, Pallas kernels, fused(): pl.pallas_call(functools.partial(fused_kernel, sizes), out_shape=results,...  267 us

profile of v8, /device:TPU:0, one launch (start us, length us, event | category | flops | bytes accessed | tf_op | source)
XLA Modules:
  0.0 272.7 jit_solution(6796227955615743800)
XLA Ops:
  0.6 266.9 %shard_map.178 = (bf16[2,2,128,1152]{3,2,1,0:T(8,128)(2,1)}, bf16[2,2,128,1152]{3,2,1,0:T(8,128)(2,1)}, f32[4,144]{1,0:T(4,128)}, f32[2,32]{1,0:T(2,128)}, f32[1...) custom-call(bf16[512,1152]{1,0:T(8,128)(2,1)} %bitcast.4, ...), custom_call_target="tpu_custom_call" | custom-call | tf_op jit(solution)/shard_map/pallas_call | solution.py:1145
  267.6 4.9 %shard_map.179 = (bf16[2,2,128,1152]{3,2,1,0:T(8,128)(2,1)}, bf16[2,2,128,1152]{3,2,1,0:T(8,128)(2,1)}, f32[4,144]{1,0:T(4,128)}, f32[2,32]{1,0:T(2,128)}, f32[1...) custom-call(bf16[2,2,128,1152]{3,2,1,0:T(8,128)(2,1)} %get-tuple-ele, ...), custom_call_target="tpu_custom_call" | custom-call | tf_op jit(solution)/shard_map/pallas_call | solution.py:1156
